TPU v7x, 32 devices: a whole 2x2x4 slice. The times are simulated.
32 devices in a mesh: rep: 1, dp: 32 (over x, y, z, core).
Axes of the slice: x: 2, y: 2, z: 4, core: 2. Of those that a mesh axis runs over, the one named last changes fastest.
Arguments:
- x: bfloat16 [32, 2048, 1024], P(('rep', 'dp'))
- dy: bfloat16 [32, 2048, 1024], P(('rep', 'dp'))
- w_gate: bfloat16 [2, 1024, 3200], P(None, 'dp')
- w_up: bfloat16 [2, 1024, 3200], P(None, 'dp')
- w_down: bfloat16 [2, 3200, 1024], P(None, 'dp')
- m_w_gate: float32 [2, 1024, 3200], P(None, 'dp')
- m_w_up: float32 [2, 1024, 3200], P(None, 'dp')
- m_w_down: float32 [2, 3200, 1024], P(None, 'dp')
- v_w_gate: float32 [2, 1024, 3200], P(None, 'dp')
- v_w_up: float32 [2, 1024, 3200], P(None, 'dp')
- v_w_down: float32 [2, 3200, 1024], P(None, 'dp')
Outputs:
- output 1: bfloat16 [2, 1024, 3200], P('rep', 'dp')
- output 2: bfloat16 [2, 1024, 3200], P('rep', 'dp')
- output 3: bfloat16 [2, 3200, 1024], P('rep', 'dp')
- output 4: float32 [2, 1024, 3200], P('rep', 'dp')
- output 5: float32 [2, 1024, 3200], P('rep', 'dp')
- output 6: float32 [2, 3200, 1024], P('rep', 'dp')
- output 7: float32 [2, 1024, 3200], P('rep', 'dp')
- output 8: float32 [2, 1024, 3200], P('rep', 'dp')
- output 9: float32 [2, 3200, 1024], P('rep', 'dp')
All inputs are finite; a program needn't handle non-finite values.
Results may differ from a plain program's by a relative error of at most 0.0279.
Values are sent between devices in bfloat16 or wider.
A program may use at most 2 GiB of HBM per device.

v0:
```python
import jax
import jax.numpy as jnp
from jax import lax
from jax.sharding import PartitionSpec as P

NAMES = ("w_gate", "w_up", "w_down")


def matmul(a, w):
    return jnp.dot(a, w, preferred_element_type=jnp.float32).astype(jnp.bfloat16)


def normed(h):
    wide = h.astype(jnp.float32)
    scale = lax.rsqrt(jnp.mean(wide**2, -1, keepdims=True) + 1e-6)
    return (wide * scale).astype(jnp.bfloat16)


def layer(h, w):
    a = normed(h)
    gate = jnp.dot(a, w["w_gate"], preferred_element_type=jnp.float32)
    up = jnp.dot(a, w["w_up"], preferred_element_type=jnp.float32)
    return h + matmul((jax.nn.silu(gate) * up).astype(jnp.bfloat16), w["w_down"])


def adamw(w, m, v, g):
    m = 0.9 * m + 0.1 * g
    v = 0.95 * v + 0.05 * g * g
    step = m * lax.rsqrt(v + 1e-8) + 0.1 * w
    return (w - 0.02 * step).astype(jnp.bfloat16), m, v


def clipped(gradients, sum_of_squares, count):
    factor = jnp.minimum(1.0, 0.5 * lax.rsqrt(sum_of_squares / count + 1e-30))
    return [g * factor for g in gradients]


def solution(mesh):
    def fetched(weights, number):
        return {name: lax.all_gather(w[number], "dp", axis=0, tiled=True) for name, w in zip(NAMES, weights, strict=True)}

    def step(x, dy, *arrays):
        weights, m, v = (arrays[i : i + 3] for i in (0, 3, 6))
        layers = weights[0].shape[0]
        h, kept = x[0], []
        for number in range(layers):
            kept.append(h)
            h = layer(h, fetched(weights, number))
        by_h, mine = dy[0], [None] * layers
        for number in reversed(range(layers)):
            _, back = jax.vjp(lambda w, h: layer(h, w), fetched(weights, number), kept[number])
            by_w, by_h = back(by_h)
            mine[number] = [lax.psum_scatter(by_w[name], "dp", scatter_dimension=0, tiled=True) for name in NAMES]
        gradients = [jnp.stack([mine[number][i] for number in range(layers)]).astype(jnp.float32) for i in range(3)]
        squares = lax.psum(sum(jnp.sum(g * g) for g in gradients), "dp")
        gradients = clipped(gradients, squares, lax.psum(1, "dp") * sum(g.size for g in gradients))
        new = [adamw(w.astype(jnp.float32), m, v, g) for w, m, v, g in zip(weights, m, v, gradients, strict=True)]
        return tuple(one[which] for which in range(3) for one in new)

    states, cut = P(("rep", "dp"), None, None), P(None, "dp", None)
    return jax.shard_map(
        step,
        mesh=mesh,
        in_specs=(states, states) + (cut,) * 9,
        out_specs=(P("rep", "dp", None),) * 9,
        check_vma=False,
    )
```

profile of v0, /device:TPU:0, one launch (start us, length us, event | category | flops | bytes accessed | tf_op | source)
XLA Modules:
  0.0 1313.1 jit_solution(13043603516952296754)
XLA Ops:
  7.2 1.8 fusion.100
  9.1 1.8 fusion.99
  11.0 2.7 fusion.98
  14.4 0.5 all-gather.23.cloned.1.call-update
  15.5 6.5 copy.38
  22.1 3.1 fusion.17
  25.1 6.5 copy.39
  31.7 52.8 %all-gather.13.cloned.1.call-done = bf16[1,1024,3200]{2,1,0:T(8,128)(2,1)} async-done(((bf16[1,32,3200]{2,1,0:T(8,128)(2,1)}), bf16[1,1024,3200]{2,1,0:T(8,128)(2,1)}) %all-gather.13.cloned.1.call-update) | async-done | bytes 6553616 | tf_op jit(solution)/shard_map/all_gather | solution.py:40
  84.5 22.8 %fusion.44 = f32[2048,3200]{1,0:T(8,128)} fusion(bf16[1,1024,3200]{2,1,0:T(8,128)(2,1)} %all-gather.13.cloned.1.call-done, bf16[1,2048,1024]{1,2,0:T(8,128)(2,1)} %copy.38, f32[2048]{0:T(1024)S(1)} %add_rsqrt_fusion), kind=kOutput, calls=%fused_computation.60 | convolution fusion | flops 13428064256 | bytes 36970496 | tf_op jit(solution)/shard_map/dot_general | solution.py:21
  107.3 49.7 %all-gather.15.cloned.1.call-done = bf16[1,1024,3200]{2,1,0:T(8,128)(2,1)} async-done(((bf16[1,32,3200]{2,1,0:T(8,128)(2,1)}), bf16[1,1024,3200]{2,1,0:T(8,128)(2,1)}) %all-gather.15.cloned.1.call-update) | async-done | bytes 6553616 | tf_op jit(solution)/shard_map/all_gather | solution.py:40
  157.0 31.3 %multiply_convert_fusion.1 = (bf16[2048,3200]{1,0:T(8,128)(2,1)}, f32[2048,3200]{1,0:T(8,128)}) fusion(f32[2048,3200]{1,0:T(8,128)} %fusion.44, bf16[1,1024,3200]{2,1,0:T(8,128)(2,1)} %all-gather.15.cloned.1.call-done, bf16[1,2048,1024]{1,2,0:T(8,128)(2,1)} %copy.38, f32[2048]{0:T(1024)S(1)} %add_rsqrt_fusion), kind=kOutput, calls=%fused_computation.17 | convolution fusion | flops 13467385856 | bytes 76292096 | tf_op jit(solution)/shard_map/dot_general | solution.py:22
  188.4 69.0 %all-gather.17.cloned.1.call-done = bf16[1,3200,1024]{2,0,1:T(2,128)(2,1)} async-done(((bf16[1,100,1024]{2,0,1:T(2,128)(2,1)}), bf16[1,3200,1024]{2,0,1:T(2,128)(2,1)}) %all-gather.17.cloned.1.call-update) | async-done | bytes 6553616 | tf_op jit(solution)/shard_map/all_gather | solution.py:40
  257.3 22.3 %fusion.21 = (f32[2048]{0:T(1024)S(1)}, bf16[2048,1024]{0,1:T(8,128)(2,1)}) fusion(bf16[2048,3200]{1,0:T(8,128)(2,1)} %get-tuple-element.55, bf16[1,3200,1024]{2,0,1:T(2,128)(2,1)} %all-gather.17.cloned.1.call-done, bf16[1,2048,1024]{1,2,0:T(8,128)(2,1)} %copy.38), kind=kOutput, calls=%fused_computation.37 | convolution fusion | flops 13432256512 | bytes 28057600 | tf_op jit(solution)/shard_map/dot_general | solution.py:10
  279.7 0.6 copy-done.14
  280.3 76.6 %all-gather.21.cloned.1.call-done = bf16[1,3200,1024]{2,0,1:T(2,128)(2,1)} async-done(((bf16[1,100,1024]{2,0,1:T(2,128)(2,1)}), bf16[1,3200,1024]{2,0,1:T(2,128)(2,1)}) %all-gather.21.cloned.1.call-update) | async-done | bytes 6553616 | tf_op jit(solution)/shard_map/all_gather | solution.py:40
  356.9 22.9 %convolution_convert_fusion.1 = bf16[2048,3200]{1,0:T(8,128)(2,1)} fusion(bf16[1,3200,1024]{2,0,1:T(2,128)(2,1)} %all-gather.21.cloned.1.call-done, bf16[1,2048,1024]{2,1,0:T(8,128)(2,1)} %param.12), kind=kOutput, calls=%fused_computation.23 | convolution fusion | flops 13428326400 | bytes 23855104 | tf_op jit(solution)/shard_map/transpose(jvp())/dot_general | solution.py:10
  379.7 48.9 %all-gather.23.cloned.1.call-done = bf16[1,1024,3200]{2,1,0:T(8,128)(2,1)} async-done(((bf16[1,32,3200]{2,1,0:T(8,128)(2,1)}), bf16[1,1024,3200]{2,1,0:T(8,128)(2,1)}) %all-gather.23.cloned.1.call-update) | async-done | bytes 6553616 | tf_op jit(solution)/shard_map/all_gather | solution.py:40
  428.6 23.4 %fusion.35 = f32[2048,3200]{1,0:T(8,128)} fusion(bf16[1,1024,3200]{2,1,0:T(8,128)(2,1)} %all-gather.23.cloned.1.call-done, bf16[2048,1024]{0,1:T(8,128)(2,1)} %get-tuple-element.58, f32[2048]{0:T(1024)S(1)} %fusion.85), kind=kOutput, calls=%fused_computation.51 | convolution fusion | flops 13428064256 | bytes 36970496 | tf_op jit(solution)/shard_map/jvp()/dot_general | solution.py:22
  452.0 49.1 %all-gather.19.cloned.1.call-done = bf16[1,1024,3200]{2,1,0:T(8,128)(2,1)} async-done(((bf16[1,32,3200]{2,1,0:T(8,128)(2,1)}), bf16[1,1024,3200]{2,1,0:T(8,128)(2,1)}) %all-gather.19.cloned.1.call-update) | async-done | bytes 6553616 | tf_op jit(solution)/shard_map/all_gather | solution.py:40
  501.1 38.5 %fusion.4 = (bf16[2048,3200]{1,0:T(8,128)(2,1)}, f32[2048,3200]{1,0:T(8,128)}) fusion(f32[2048,3200]{1,0:T(8,128)} %fusion.35, bf16[2048,3200]{1,0:T(8,128)(2,1)} %convolution_convert_fusion.1, bf16[1,1024,3200]{2,1,0:T(8,128)(2,1)} %all-gather.19.cloned.1.call-done, bf16[2048,1024]{0,1:T(8,128)(2,1)} %get-tuple-element.58, f32[2048]{0:T(1024)S(1)} %fusion.85), kind=kOutput, calls=%fused_computation.8 | convolution fusion | flops 13506707456 | bytes 89399296 | tf_op jit(solution)/shard_map/jvp()/dot_general | solution.py:21
  539.6 22.6 %fusion.14 = bf16[2048,1024]{0,1:T(8,128)(2,1)} fusion(bf16[2048,3200]{1,0:T(8,128)(2,1)} %convolution_convert_fusion.1, bf16[1,1024,3200]{2,1,0:T(8,128)(2,1)} %all-gather.23.cloned.1.call-done, f32[2048,3200]{1,0:T(8,128)} %get-tuple-element.60), kind=kOutput, calls=%fused_computation.21 | convolution fusion | flops 13461094400 | bytes 50069504 | tf_op jit(solution)/shard_map/transpose(jvp())/dot_general | solution.py:22
  562.2 19.7 %fusion.23 = (f32[2048]{0:T(1024)S(1)}, bf16[2048,1024]{0,1:T(8,128)(2,1)S(1)}) fusion(bf16[2048,1024]{0,1:T(8,128)(2,1)S(1)} %copy-done.1, bf16[2048,1024]{0,1:T(8,128)(2,1)} %fusion.14, bf16[2048,3200]{1,0:T(8,128)(2,1)} %get-tuple-element.59, bf16[1,1024,3200]{2,1,0:T(8,128)(2,1)} %all-gather.19.cloned.1.call-done), kind=kOutput, calls=%fused_computation.39 | convolution fusion | flops 13432256512 | bytes 32251904 | tf_op jit(solution)/shard_map/transpose(jvp())/dot_general | solution.py:21
  582.0 5.0 fusion.47
  587.0 22.9 %convolution_convert_fusion = bf16[2048,3200]{1,0:T(8,128)(2,1)} fusion(bf16[2048,1024]{0,1:T(8,128)(2,1)} %fusion.47, bf16[1,3200,1024]{2,0,1:T(2,128)(2,1)} %all-gather.17.cloned.1.call-done), kind=kOutput, calls=%fused_computation.22 | convolution fusion | flops 13428326400 | bytes 23855104 | tf_op jit(solution)/shard_map/transpose(jvp())/dot_general | solution.py:10
  609.9 25.6 %fusion.29 = bf16[1024,3200]{1,0:T(8,128)(2,1)} fusion(bf16[2048,3200]{1,0:T(8,128)(2,1)} %convolution_convert_fusion, f32[2048,3200]{1,0:T(8,128)} %fusion.44, bf16[1,2048,1024]{1,2,0:T(8,128)(2,1)} %copy.38, f32[2048]{0:T(1024)S(1)} %copy-done.17), kind=kOutput, calls=%fused_computation.43 | convolution fusion | flops 13470662656 | bytes 50077696 | tf_op jit(solution)/shard_map/transpose(jvp())/dot_general | solution.py:22
  635.6 25.3 %fusion.28 = bf16[1024,3200]{1,0:T(8,128)(2,1)} fusion(bf16[2048,3200]{1,0:T(8,128)(2,1)} %convolution_convert_fusion.1, bf16[2048,1024]{0,1:T(8,128)(2,1)} %get-tuple-element.58, f32[2048]{0:T(1024)S(1)} %fusion.85, f32[2048,3200]{1,0:T(8,128)} %get-tuple-element.60), kind=kOutput, calls=%fused_computation.42 | convolution fusion | flops 13470662656 | bytes 50077696 | tf_op jit(solution)/shard_map/transpose(jvp())/dot_general | solution.py:22
  660.9 32.5 %fusion.24 = bf16[1024,3200]{1,0:T(8,128)(2,1)} fusion(f32[2048,3200]{1,0:T(8,128)} %fusion.44, f32[2048,3200]{1,0:T(8,128)} %get-tuple-element.56, bf16[2048,3200]{1,0:T(8,128)(2,1)} %convolution_convert_fusion, bf16[1,2048,1024]{1,2,0:T(8,128)(2,1)} %copy.38, f32[2048]{0:T(1024)S(1)} %copy-done.17), kind=kOutput, calls=%fused_computation.40 | convolution fusion | flops 13503430656 | bytes 76292096 | tf_op jit(solution)/shard_map/transpose(jvp())/dot_general | solution.py:21
  693.5 21.1 %convolution_convert_fusion.3 = bf16[1024,3200]{1,0:T(8,128)(2,1)} fusion(bf16[2048,3200]{1,0:T(8,128)(2,1)} %get-tuple-element.59, bf16[2048,1024]{0,1:T(8,128)(2,1)} %get-tuple-element.58, f32[2048]{0:T(1024)S(1)} %fusion.85), kind=kOutput, calls=%fused_computation.45 | convolution fusion | flops 13428064256 | bytes 23863296 | tf_op jit(solution)/shard_map/transpose(jvp())/dot_general | solution.py:21
  714.7 20.4 %convolution_convert_fusion.2 = bf16[3200,1024]{1,0:T(8,128)(2,1)} fusion(bf16[2048,3200]{1,0:T(8,128)(2,1)} %get-tuple-element.55, bf16[2048,1024]{0,1:T(8,128)(2,1)} %fusion.47), kind=kOutput, calls=%fused_computation.44 | convolution fusion | flops 13425049600 | bytes 23855104 | tf_op jit(solution)/shard_map/transpose(jvp())/dot_general | solution.py:10
  735.1 26.0 %fusion.27 = bf16[3200,1024]{1,0:T(8,128)(2,1)} fusion(f32[2048,3200]{1,0:T(8,128)} %fusion.35, bf16[1,2048,1024]{2,1,0:T(8,128)(2,1)} %param.12, f32[2048,3200]{1,0:T(8,128)} %get-tuple-element.60), kind=kOutput, calls=%fused_computation.41 | convolution fusion | flops 13464371200 | bytes 63176704 | tf_op jit(solution)/shard_map/transpose(jvp())/dot_general | solution.py:10
  761.2 239.2 %fusion.91 = (bf16[104,1024]{1,0:T(8,128)(2,1)S(1)}, bf16[104,1024]{1,0:T(8,128)(2,1)S(1)}) fusion(bf16[3200,1024]{1,0:T(8,128)(2,1)} %fusion.27, bf16[3200,1024]{1,0:T(8,128)(2,1)} %convolution_convert_fusion.2), kind=kCustom, calls=%all-reduce-scatter.2 | all-reduce-scatter fusion | flops 6815745 | bytes 13533184
  1000.4 1.4 collective-permute-start
  1001.8 2.0 collective-permute-start.2
  1003.8 2.0 collective-permute-start.1
  1005.9 1.9 collective-permute-start.3
  1008.7 1.5 collective-permute-done.3
  1010.2 1.3 concatenate.1
  1011.7 0.8 fusion.68
  1012.5 1.9 fusion.79
  1014.4 94.5 %reduce-scatter.9.cloned.1.call-done = bf16[32,3200]{1,0:T(8,128)(2,1)} async-done(((bf16[1024,3200]{1,0:T(8,128)(2,1)}), bf16[32,3200]{1,0:T(8,128)(2,1)}) %reduce-scatter.9.cloned.1.call-update) | async-done | bytes 204816 | tf_op jit(solution)/shard_map/reduce_scatter | solution.py:53
  1108.8 146.7 %reduce-scatter.11.cloned.1.call-done = bf16[32,3200]{1,0:T(8,128)(2,1)} async-done(((bf16[1024,3200]{1,0:T(8,128)(2,1)}), bf16[32,3200]{1,0:T(8,128)(2,1)}) %reduce-scatter.11.cloned.1.call-update) | async-done | bytes 204816 | tf_op jit(solution)/shard_map/reduce_scatter | solution.py:53
  1255.5 1.9 fusion.78
  1259.4 36.9 %psum.7 = f32[]{:T(128)} all-reduce(f32[]{:T(128)S(6)} %add.99), channel_id=1, replica_groups=mesh['rep'=1,'dp'=32] {'dp'}, use_global_device_ids=true, to_apply=%region_12.13 | all-reduce | flops 1 | bytes 8 | tf_op jit(solution)/shard_map/psum | solution.py:55
  1297.0 2.2 fusion.71
  1299.2 1.5 copy.44
  1300.7 1.5 copy.45
  1302.3 1.2 copy.43
  1303.5 2.4 fusion.77
  (67 shorter events, 2.6 us)
Async XLA Ops:
  7.2 77.3 %all-gather.13.cloned.1.call-start = ((), (), s32[]{:S(2)}) async-start(), calls=%async_computation.8 | async-start | bytes 6758400 | tf_op jit(solution)/shard_map/all_gather | solution.py:40
  9.1 148.0 %all-gather.15.cloned.1.call-start = ((), (), s32[]{:S(2)}) async-start(), calls=%async_computation.9 | async-start | bytes 6758400 | tf_op jit(solution)/shard_map/all_gather | solution.py:40
  10.9 246.4 %all-gather.17.cloned.1.call-start = ((), (), s32[]{:S(2)}) async-start(), calls=%async_computation.10 | async-start | bytes 13516800 | tf_op jit(solution)/shard_map/all_gather | solution.py:40
  13.7 343.1 %all-gather.21.cloned.1.call-start = ((), (), s32[]{:S(2)}) async-start(), calls=%async_computation.12 | async-start | bytes 13516800 | tf_op jit(solution)/shard_map/all_gather | solution.py:40
  14.3 414.3 %all-gather.23.cloned.1.call-start = ((), (), s32[]{:S(2)}) async-start(), calls=%async_computation.13 | async-start | bytes 6758400 | tf_op jit(solution)/shard_map/all_gather | solution.py:40
  14.9 486.2 %all-gather.19.cloned.1.call-start = ((), (), s32[]{:S(2)}) async-start(), calls=%async_computation.11 | async-start | bytes 6758400 | tf_op jit(solution)/shard_map/all_gather | solution.py:40
  15.5 997.0 %reduce-scatter.13.cloned.1.call-start = ((), (), s32[]{:S(2)}) async-start(), calls=%async_computation.6 | async-start | bytes 6758400 | tf_op jit(solution)/shard_map/reduce_scatter | solution.py:53
  25.1 131.9 %copy-start.16 = (f32[2048]{0:T(1024)}, f32[2048]{0:T(1024)S(1)}, u32[]{:S(2)}) copy-start(f32[2048]{0:T(1024)S(1)} %add_rsqrt_fusion) | copy-start | bytes 24580
  279.7 0.6 copy-start.14
  539.6 22.6 %copy-start.1 = (bf16[2048,1024]{0,1:T(8,128)(2,1)S(1)}, bf16[2048,1024]{0,1:T(8,128)(2,1)}, u32[]{:S(2)}) copy-start(bf16[2048,1024]{0,1:T(8,128)(2,1)} %get-tuple-element.58) | copy-start | bytes 12582916
  562.2 19.7 %copy-start.15 = (f32[2048]{0:T(1024)S(1)}, f32[2048]{0:T(1024)}, u32[]{:S(2)}) copy-start(f32[2048]{0:T(1024)} %copy-done.14) | copy-start | bytes 24580
  562.2 19.8 %copy-start = (bf16[1,2048,1024]{1,2,0:T(8,128)(2,1)S(1)}, bf16[1,2048,1024]{1,2,0:T(8,128)(2,1)}, u32[]{:S(2)}) copy-start(bf16[1,2048,1024]{1,2,0:T(8,128)(2,1)} %copy.39) | copy-start | bytes 12582916
  587.0 22.9 %copy-start.17 = (f32[2048]{0:T(1024)S(1)}, f32[2048]{0:T(1024)}, u32[]{:S(2)}) copy-start(f32[2048]{0:T(1024)} %copy-done.16) | copy-start | bytes 24580
  635.5 377.0 %reduce-scatter.15.cloned.1.call-start = ((), (), s32[]{:S(2)}) async-start(), calls=%async_computation.7 | async-start | bytes 6758400 | tf_op jit(solution)/shard_map/reduce_scatter | solution.py:53
  660.9 448.0 %reduce-scatter.9.cloned.1.call-start = ((), (), s32[]{:S(2)}) async-start(), calls=%async_computation.4 | async-start | bytes 6758400 | tf_op jit(solution)/shard_map/reduce_scatter | solution.py:53
  693.5 562.1 %reduce-scatter.11.cloned.1.call-start = ((), (), s32[]{:S(2)}) async-start(), calls=%async_computation.5 | async-start | bytes 6758400 | tf_op jit(solution)/shard_map/reduce_scatter | solution.py:53
  761.2 535.8 %copy-start.2 = (bf16[2,100,1024]{2,0,1:T(2,128)(2,1)S(1)}, bf16[2,100,1024]{2,0,1:T(2,128)(2,1)}, u32[]{:S(2)}) copy-start(bf16[2,100,1024]{2,0,1:T(2,128)(2,1)} %param.15) | copy-start | bytes 1228804
  761.2 535.8 %copy-start.9 = (f32[2,100,1024]{2,0,1:T(2,128)S(1)}, f32[2,100,1024]{2,0,1:T(2,128)}, u32[]{:S(2)}) copy-start(f32[2,100,1024]{2,0,1:T(2,128)} %param.21) | copy-start | bytes 2457604
  1000.4 303.1 %copy-start.3 = (bf16[2,32,3200]{2,1,0:T(8,128)(2,1)S(1)}, bf16[2,32,3200]{2,1,0:T(8,128)(2,1)}, u32[]{:S(2)}) copy-start(bf16[2,32,3200]{2,1,0:T(8,128)(2,1)} %param.13) | copy-start | bytes 1228804
  1000.4 303.1 %copy-start.4 = (bf16[2,32,3200]{2,1,0:T(8,128)(2,1)S(1)}, bf16[2,32,3200]{2,1,0:T(8,128)(2,1)}, u32[]{:S(2)}) copy-start(bf16[2,32,3200]{2,1,0:T(8,128)(2,1)} %param.14) | copy-start | bytes 1228804
  1000.4 7.8 collective-permute-start
  1001.8 8.4 collective-permute-start.2
  1003.8 4.3 collective-permute-start.1
  1005.9 4.3 collective-permute-start.3
  1012.5 290.9 %copy-start.5 = (bf16[32,3200]{1,0:T(8,128)(2,1)S(1)}, bf16[32,3200]{1,0:T(8,128)(2,1)}, u32[]{:S(2)}) copy-start(bf16[32,3200]{1,0:T(8,128)(2,1)} %reduce-scatter.13.cloned.1.call-done) | copy-start | bytes 614404
  1012.5 290.9 %copy-start.6 = (bf16[32,3200]{1,0:T(8,128)(2,1)S(1)}, bf16[32,3200]{1,0:T(8,128)(2,1)}, u32[]{:S(2)}) copy-start(bf16[32,3200]{1,0:T(8,128)(2,1)} %reduce-scatter.15.cloned.1.call-done) | copy-start | bytes 614404
  1108.8 194.6 %copy-start.7 = (bf16[32,3200]{1,0:T(8,128)(2,1)S(1)}, bf16[32,3200]{1,0:T(8,128)(2,1)}, u32[]{:S(2)}) copy-start(bf16[32,3200]{1,0:T(8,128)(2,1)} %reduce-scatter.9.cloned.1.call-done) | copy-start | bytes 614404
  1255.5 47.9 %copy-start.8 = (bf16[32,3200]{1,0:T(8,128)(2,1)S(1)}, bf16[32,3200]{1,0:T(8,128)(2,1)}, u32[]{:S(2)}) copy-start(bf16[32,3200]{1,0:T(8,128)(2,1)} %reduce-scatter.11.cloned.1.call-done) | copy-start | bytes 614404
  1296.9 6.5 copy-start.10
  1297.0 6.5 copy-start.11
  1297.0 6.5 copy-start.12
  1297.0 6.5 copy-start.13
Sparse Core Ops, SparseCore 0:
  11.4 72.9 all-gather.12
  87.9 69.0 all-gather.14
  160.5 96.8 all-gather.16
  260.6 96.1 all-gather.20
  360.1 68.4 all-gather.22
  431.9 69.0 all-gather.18
  635.7 147.8 reduce-scatter.12
  785.8 168.4 reduce-scatter.14
  956.6 152.1 reduce-scatter.8
  1111.0 144.4 reduce-scatter.10
where the time goes:
time: 1320 us; the launch traced here: 1310 us
  waiting for transfers between devices  591 us (45%)
  matrix products  378 us (29%)
  blocking collectives  276 us (21%)
  local copies, waits for them, and re-layouts  26.3 us (2%)
  between operations  17.5 us (1%)
  other arithmetic  17.3 us (1%)
    all_gather x6, waiting for transfers between devices, fetched(): lax.all_gather(w[number], 'dp', axis=0, tiled=True)  346 us
    reduce_scatter x4, waiting for transfers between devices, step(): lax.psum_scatter(by_w[name], 'dp', scatter_dimension=0, tiled=True)  241 us
    unnamed x1, blocking collectives  239 us
    dot_general x5, matrix products, layer(): gate = jnp.dot(a, w['w_gate'], preferred_element_type=jnp.float32)  135 us
    dot_general x5, matrix products, layer(): up = jnp.dot(a, w['w_up'], preferred_element_type=jnp.float32)  128 us
    dot_general x5, matrix products, matmul(): jnp.dot(a, w, preferred_element_type=jnp.float32).astype(jnp.bfloat16)  115 us
    psum x1, blocking collectives, step(): squares = lax.psum(sum((jnp.sum(g * g) for g in gradients)), 'dp')  36.9 us
  transfers between devices with their start and end apart: 14, of which 10 were waited for; matrix products, arithmetic and copies ran while one was open for 39% of the time, Pallas kernels for 0%

commit v1 on v0

v1 whole, which is shorter than its diff:
```python
import jax
import jax.numpy as jnp
from jax import lax
from jax.experimental import pallas as pl
from jax.experimental.pallas import tpu as pltpu
from jax.sharding import PartitionSpec as P

T, D, F = 2048, 1024, 3200
BF, F32 = jnp.bfloat16, jnp.float32
ANY = pl.BlockSpec(memory_space=pl.ANY)
NT = (((1,), (1,)), ((), ()))
TN = (((0,), (0,)), ((), ()))

X, Y, ZH, ZL, C = 16, 8, 4, 2, 1
R = {X: 2, Y: 1}


def normed(h):
    wide = h.astype(F32)
    scale = lax.rsqrt(jnp.mean(wide**2, -1, keepdims=True) + 1e-6)
    return (wide * scale).astype(BF)


def cost(flops, moved, trans=0):
    return pl.CostEstimate(flops=flops, bytes_accessed=moved, transcendentals=trans)


def peer(bits):
    index = lax.axis_index("dp")
    there = index
    for bit in (X, Y, ZH, ZL, C):
        if bits & bit:
            there = there + bit - 2 * bit * ((index // bit) % 2)
    return there


def at_peer(bits, low, high):
    return (peer(bits) // low) % (2 * high // low)


class Gather:
    def __init__(self, own, shape, rounds, steps, home):
        self.home = home
        self.ins, self.outs, self.rounds, self.steps = [own], [jax.ShapeDtypeStruct(shape, BF)], rounds, steps
        self.scratch = [pltpu.VMEM(own.shape, BF), pltpu.SemaphoreType.DMA]

    def place(self, ins, outs, scratch):
        staged, sem = scratch
        dst = self.home(outs[0])
        for pair in ((ins[0], staged), (staged, dst)):
            copy = pltpu.make_async_copy(*pair, sem)
            copy.start()
            copy.wait()


def wide_gather(own, first, second, steps):
    a, b = R[first], R[second]

    def rounds(ins, outs):
        (own,), (buf,) = ins, outs
        part = lambda r, k: buf.at[r, k]
        return [
            [(own, buf.at[0, 0, at_peer(0, ZL, ZH)], 2 * j) for j in (1, 2, 3)],
            [(part(0, 0), part(a, 0), first), (part(0, 0), part(b, 0), second), (part(0, 0), part(0, 1), C)],
            [(part(a, 0), part(3, 0), second), (part(a, 0), part(a, 1), C), (part(b, 0), part(b, 1), C)],
            [(part(3, 0), part(3, 1), C)],
        ]

    return Gather(own, (4, 2, 4, 32, F), rounds, steps, lambda buf: buf.at[0, 0, at_peer(0, ZL, ZH)])


def down_gather(own, first, second, steps):
    a, b = R[first], R[second]

    def rounds(ins, outs):
        (own,), (buf,) = ins, outs
        part = lambda l, k, r: buf.at[l, k, r]
        across = lambda l, *rs: [(part(l, 0, r), part(l, 1, r), C) for r in rs]
        over = lambda *rs: [(part(0, 0, r), part(1, 0, r), ZL) for r in rs]
        return [
            [(own, buf.at[0, 0, 0, at_peer(0, ZH, ZH)], ZH)],
            [(part(0, 0, 0), part(0, 0, a), first), (part(0, 0, 0), part(0, 0, b), second)] + over(0) + across(0, 0),
            [(part(0, 0, a), part(0, 0, 3), second)] + over(a, b) + across(0, a, b) + across(1, 0),
            over(3) + across(0, 3) + across(1, a, b),
            across(1, 3),
        ]

    return Gather(own, (2, 2, 4, 2, 400, 256), rounds, steps, lambda buf: buf.at[0, 0, 0, at_peer(0, ZH, ZH)])


class Swap:
    def __init__(self, *pairs, step=0):
        self.ins = [a for a, _ in pairs]
        self.outs = [jax.ShapeDtypeStruct(a.shape, a.dtype) for a in self.ins]
        self.rounds = lambda ins, outs: [[(s, d, bits) for s, d, (_, bits) in zip(ins, outs, pairs)]]
        self.steps, self.scratch = [step], []

    def place(self, ins, outs, scratch):
        pass


class Finish(Swap):
    def __init__(self, parts, first, second, steps):
        self.ins, self.steps, self.scratch = [parts[first], parts[second]], steps, []
        self.outs = [jax.ShapeDtypeStruct((4, 32, F), BF)] * 4
        self.rounds = lambda i, o: [[(i[0], o[0], second), (i[0], o[1], C), (i[1], o[2], C)], [(o[0], o[3], C)]]


def run(body, comms, *, grid, ins, in_specs, outs, out_specs, scratch, number, name, estimate=None):
    n_in, n_out, n_scratch = len(ins), len(outs), len(scratch)
    counts = [(len(c.ins), len(c.outs), len(c.scratch)) for c in comms]
    total = 1
    for n in grid:
        total *= n

    def take(refs, which, start):
        found, at = [], start
        for count in counts:
            found.append(refs[at : at + count[which]])
            at += count[which]
        return found, at

    def kernel(*refs):
        mine_in = refs[:n_in]
        their_ins, at = take(refs, 0, n_in)
        mine_out, at = refs[at : at + n_out], at + n_out
        their_outs, at = take(refs, 1, at)
        mine_scratch, at = refs[at : at + n_scratch], at + n_scratch
        their_scratch, at = take(refs, 2, at)
        send, recv = refs[at:] if comms else (None, None)
        copies, used, bits = [], 0, []
        for c, i, o in zip(comms, their_ins, their_outs):
            per = []
            for one in c.rounds(i, o):
                here = []
                for source, target, b in one:
                    here.append((source, target, b, used))
                    used += 1
                    if b not in bits:
                        bits.append(b)
                per.append(here)
            copies.append(per)

        def make(item):
            source, target, b, n = item
            return pltpu.make_async_remote_copy(
                src_ref=source, dst_ref=target, send_sem=send.at[n], recv_sem=recv.at[n],
                device_id={"dp": peer(b)}, device_id_type=pl.DeviceIdType.MESH,
            )

        events = sorted((s, n, p) for p, c in enumerate(comms) for n, s in enumerate(c.steps))
        if not grid:
            step = 0
        else:
            step = pl.program_id(0)
            for d in range(1, len(grid)):
                step = step * grid[d] + pl.program_id(d)

        def enter():
            barrier = pltpu.get_barrier_semaphore()
            for b in bits:
                pl.semaphore_signal(barrier, inc=1, device_id={"dp": peer(b)}, device_id_type=pl.DeviceIdType.MESH)
            for c, i, o, s in zip(comms, their_ins, their_outs, their_scratch):
                c.place(i, o, s)
            pl.semaphore_wait(barrier, len(bits))

        def advance(now):
            for s, n, p in events:
                if s == now:
                    if n:
                        for item in copies[p][n - 1]:
                            make(item).wait()
                    for item in copies[p][n]:
                        make(item).start()

        def leave():
            for p, c in enumerate(comms):
                for item in copies[p][-1]:
                    make(item).wait()

        if not comms:
            return body(mine_in, mine_out, mine_scratch)
        times = sorted({s for s, _, _ in events})
        if not grid:
            enter()
            for t in times:
                advance(t)
            leave()
            return
        for t in times:

            @pl.when(step == t)
            def _():
                if t == 0:
                    enter()
                advance(t)

        body(mine_in, mine_out, mine_scratch)

        @pl.when(step == total - 1)
        def _():
            leave()

    n_copies = 0
    for c in comms:
        fake = lambda shapes: [Shape(s.shape) for s in shapes]
        n_copies += sum(len(one) for one in c.rounds(fake(c.ins), fake(c.outs)))
    all_scratch = list(scratch) + [s for c in comms for s in c.scratch]
    if comms:
        all_scratch += [pltpu.SemaphoreType.DMA((n_copies,))] * 2
    n_comm_in, n_comm_out = sum(c[0] for c in counts), sum(c[1] for c in counts)
    call = pl.pallas_call(
        kernel,
        grid=grid,
        in_specs=list(in_specs) + [ANY] * n_comm_in,
        out_specs=list(out_specs) + [ANY] * n_comm_out,
        out_shape=list(outs) + [s for c in comms for s in c.outs],
        scratch_shapes=all_scratch,
        compiler_params=pltpu.CompilerParams(collective_id=number, has_side_effects=True) if comms else pltpu.CompilerParams(),
        cost_estimate=estimate,
        name=name,
    )
    return call, (*ins, *[a for c in comms for a in c.ins])


class Shape:
    def __init__(self, shape):
        self.shape, self.at = shape, self

    def __getitem__(self, _):
        return self


def wide_copies(pieces, slot, sem, columns, place):
    for r in range(4):
        for k in range(2):
            piece = pieces[2 * r + k] if len(pieces) == 8 else pieces[0].at[r, k]
            yield pltpu.make_async_copy(piece.at[:, :, columns], slot.at[at_peer(r * Y, Y, X), :, at_peer(k, C, C), :, place], sem)


def down_copies(pieces, slot, sem):
    for l in range(2):
        for k in range(2):
            columns = pl.ds(pl.multiple_of(at_peer(l * ZL + k, C, ZL) * 256, 256), 256)
            for r in range(4):
                yield pltpu.make_async_copy(pieces.at[l, k, r], slot.at[at_peer(r * Y, Y, X), :, :, columns], sem)


def struct(shape, dtype=BF):
    return jax.ShapeDtypeStruct(shape, dtype)


def gate_up(a, gate_w, up_w, comms, number):
    blocks, chunks, rows = 5, 5, 512

    def body(ins, outs, scratch):
        a_ref, *w_refs = ins
        g_ref, u_ref = w_refs[: len(gate_w)], w_refs[len(gate_w) :]
        act_ref, s_ref, t_ref = outs
        slots, sems = scratch
        n, m = pl.program_id(0), pl.program_id(1)

        def copies(block, slot):
            start = pl.multiple_of(block * chunks * 128, 128)
            for k, pieces in enumerate((g_ref, u_ref)):
                yield from wide_copies(pieces, slots.at[slot, k], sems.at[slot], pl.ds(start, chunks * 128), slice(None))

        now = n % 2

        @pl.when((n == 0) & (m == 0))
        def _():
            for copy in copies(0, 0):
                copy.start()

        @pl.when(m == 0)
        def _():
            for copy in copies(n, now):
                copy.wait()

            @pl.when(n + 1 < blocks)
            def _():
                for copy in copies(n + 1, 1 - now):
                    copy.start()

        lhs = a_ref[...]
        for i in range(chunks):
            w = jnp.concatenate([slots[now, k, :, :, :, :, i * 128 : i * 128 + 128].reshape(D, 128) for k in range(2)], 1)
            both = jnp.dot(lhs, w, preferred_element_type=F32)
            gate, up = both[:, :128], both[:, 128:]
            sig = 1.0 / (1.0 + jnp.exp(-gate))
            s = gate * sig
            at = slice(i * 128, i * 128 + 128)
            act_ref[:, at] = (s * up).astype(BF)
            s_ref[:, at] = s
            t_ref[:, at] = up * (sig + s * (1.0 - sig))

    out = pl.BlockSpec((rows, chunks * 128), lambda n, m: (m, n))
    call, operands = run(
        body, comms, grid=(blocks, T // rows),
        ins=[a, *gate_w, *up_w], in_specs=[pl.BlockSpec((rows, D), lambda n, m: (m, 0))] + [ANY] * len(gate_w + up_w),
        outs=[struct((T, F)), struct((T, F), F32), struct((T, F), F32)], out_specs=[out] * 3,
        scratch=[pltpu.VMEM((2, 2, 4, 4, 2, 32, chunks * 128), BF), pltpu.SemaphoreType.DMA((2,))],
        number=number, name="gate_up", estimate=cost(4 * T * D * F, T * F * 10 + 4 * D * F, T * F * 2),
    )
    return call(*operands)


def row(rows, n):
    return pl.BlockSpec((rows, n), lambda m: (m, 0))


def fetch_down(p_ref, w_ref, sem):
    @pl.when(pl.program_id(0) == 0)
    def _():
        for copy in down_copies(p_ref, w_ref, sem):
            copy.start()
        for copy in down_copies(p_ref, w_ref, sem):
            copy.wait()


def down(act, h, pieces, comms, number):
    def body(ins, outs, scratch):
        act_ref, h_ref, p_ref = ins
        fetch_down(p_ref, *scratch)
        out = h_ref[...] + jnp.dot(act_ref[...], scratch[0][...].reshape(F, D), preferred_element_type=F32).astype(BF)
        outs[0][...] = out
        outs[1][...] = normed(out)

    call, operands = run(
        body, comms, grid=(T // 256,), ins=[act, h, pieces], in_specs=[row(256, F), row(256, D), ANY],
        outs=[struct((T, D))] * 2, out_specs=[row(256, D)] * 2, scratch=[pltpu.VMEM((4, 2, 400, D), BF), pltpu.SemaphoreType.DMA],
        number=number, name="down", estimate=cost(2 * T * D * F, T * F * 2 + T * D * 6 + 2 * D * F),
    )
    return call(*operands)


def by_hidden(dh, s, t, pieces, comms, number):
    def body(ins, outs, scratch):
        dh_ref, s_ref, t_ref, p_ref = ins
        dg_ref, du_ref = outs
        w_ref = scratch[0]
        fetch_down(p_ref, *scratch)
        lhs = dh_ref[...]
        w = w_ref[...].reshape(F, D)
        for at in range(0, F, 640):
            at = slice(at, at + 640)
            d = lax.dot_general(lhs, w[at, :], NT, preferred_element_type=F32).astype(BF).astype(F32)
            du_ref[:, at] = (d * s_ref[:, at]).astype(BF)
            dg_ref[:, at] = (d * t_ref[:, at]).astype(BF)

    call, operands = run(
        body, comms, grid=(T // 256,), ins=[dh, s, t, pieces], in_specs=[row(256, D), row(256, F), row(256, F), ANY],
        outs=[struct((T, F))] * 2, out_specs=[row(256, F)] * 2, scratch=[pltpu.VMEM((4, 2, 400, D), BF), pltpu.SemaphoreType.DMA],
        number=number, name="by_hidden", estimate=cost(2 * T * D * F, T * F * 12 + T * D * 2 + 2 * D * F),
    )
    return call(*operands)


def by_input(dg, du, dh, h, gate_w, up_w, comms, number):
    def body(ins, outs, scratch):
        dg_ref, du_ref, dh_ref, h_ref, *w_refs = ins
        g_ref, u_ref = w_refs[: len(gate_w)], w_refs[len(gate_w) :]
        slots, sems = scratch

        @pl.when(pl.program_id(0) == 0)
        def _():
            both = [c for k, p in enumerate((g_ref, u_ref)) for c in wide_copies(p, slots.at[k], sems.at[k], slice(None), slice(None))]
            for copy in both:
                copy.start()
            for copy in both:
                copy.wait()

        halves = []
        for k, d_ref in enumerate((dg_ref, du_ref)):
            w = slots[k].reshape(D, F)
            halves.append(lax.dot_general(d_ref[...], w, NT, preferred_element_type=F32).astype(BF))
        da = (halves[0] + halves[1]).astype(F32)
        wide = h_ref[...].astype(F32)
        scale = lax.rsqrt(jnp.mean(wide**2, -1, keepdims=True) + 1e-6)
        along = jnp.mean(da * wide, -1, keepdims=True)
        outs[0][...] = dh_ref[...] + (da * scale - wide * (scale * scale * scale * along)).astype(BF)

    call, operands = run(
        body, comms, grid=(T // 256,), ins=[dg, du, dh, h, *gate_w, *up_w],
        in_specs=[row(256, F), row(256, F), row(256, D), row(256, D)] + [ANY] * len(gate_w + up_w),
        outs=[struct((T, D))], out_specs=[row(256, D)],
        scratch=[pltpu.VMEM((2, 4, 4, 2, 32, F), BF), pltpu.SemaphoreType.DMA((2,))],
        number=number, name="by_input", estimate=cost(4 * T * D * F, T * F * 4 + T * D * 6 + 4 * D * F),
    )
    return call(*operands)


def by_wide(at, d, comms, number):
    columns = 640

    def body(ins, outs, scratch):
        at_ref, d_ref = ins
        for k, ref in enumerate(outs):
            ref[...] = jnp.dot(at_ref[k * D // 2 : (k + 1) * D // 2, :], d_ref[...], preferred_element_type=F32).astype(BF)

    out = pl.BlockSpec((D // 2, columns), lambda n: (0, n))
    call, operands = run(
        body, comms, grid=(F // columns,), ins=[at, d],
        in_specs=[pl.BlockSpec((D, T), lambda n: (0, 0)), pl.BlockSpec((T, columns), lambda n: (0, n))],
        outs=[struct((D // 2, F))] * 2, out_specs=[out] * 2, scratch=[],
        number=number, name="by_wide", estimate=cost(2 * T * D * F, T * F * 2 + T * D * 2 + D * F * 2),
    )
    return call(*operands)


def by_down(act, dh, comms, number):
    rows = 640

    def body(ins, outs, scratch):
        act_ref, dh_ref = ins
        for n, ref in enumerate(outs):
            columns = pl.ds(pl.multiple_of(at_peer(n, C, ZL) * 256, 256), 256)
            ref[...] = lax.dot_general(act_ref[...], dh_ref[:, columns], TN, preferred_element_type=F32).astype(BF)

    call, operands = run(
        body, comms, grid=(F // rows,), ins=[act, dh],
        in_specs=[pl.BlockSpec((T, rows), lambda n: (0, n)), pl.BlockSpec((T, D), lambda n: (0, 0))],
        outs=[struct((F, 256))] * 4, out_specs=[pl.BlockSpec((rows, 256), lambda n: (n, 0))] * 4, scratch=[],
        number=number, name="by_down", estimate=cost(2 * T * D * F, T * F * 2 + T * D * 2 + D * F * 2),
    )
    return call(*operands)


def only(comms, number, name):
    call, operands = run(None, comms, grid=(), ins=[], in_specs=[], outs=[], out_specs=[], scratch=[], number=number, name=name)
    return call(*operands)


def everyone(value, number):
    groups = (tuple(range(1, 8)), (8, 16, 24))

    def kernel(value_ref, out_ref, mid_ref, slots, send, recv):
        barrier = pltpu.get_barrier_semaphore()
        for b in groups[0] + groups[1]:
            pl.semaphore_signal(barrier, inc=1, device_id={"dp": peer(b)}, device_id_type=pl.DeviceIdType.MESH)
        pl.semaphore_wait(barrier, 10)
        source, target, n = value_ref, mid_ref, 0
        for group in groups:
            copies = []
            for b in group:
                copies.append(
                    pltpu.make_async_remote_copy(
                        src_ref=source, dst_ref=slots.at[n], send_sem=send.at[n], recv_sem=recv.at[n],
                        device_id={"dp": peer(b)}, device_id_type=pl.DeviceIdType.MESH,
                    )
                )
                copies[-1].start()
                n += 1
            total = source[...]
            for i, copy in enumerate(copies):
                copy.wait()
                total = total + slots[n - len(copies) + i]
            target[...] = total
            source, target = mid_ref, out_ref

    spec = pl.BlockSpec(memory_space=pltpu.VMEM)
    return pl.pallas_call(
        kernel, in_specs=[spec], out_specs=spec, out_shape=struct((8, 128), F32),
        scratch_shapes=[pltpu.VMEM((8, 128), F32), pltpu.VMEM((10, 8, 128), F32)] + [pltpu.SemaphoreType.DMA((10,))] * 2,
        compiler_params=pltpu.CompilerParams(collective_id=number, has_side_effects=True), name="everyone",
    )(jnp.broadcast_to(value, (8, 128)))[0, 0]


def adamw(w, m, v, g):
    m = 0.9 * m + 0.1 * g
    v = 0.95 * v + 0.05 * g * g
    step = m * lax.rsqrt(v + 1e-8) + 0.1 * w
    return (w - 0.02 * step).astype(BF), m, v


def f32(a):
    return a.astype(F32)


LEFT, RIGHT = slice(0, 1664), slice(1664, F)


class WideSum:
    def __init__(self, keep, send):
        self.keep, self.send = keep.reshape(4, 4, 32, F), send.reshape(4, 4, 32, F)

    def core(self):
        return [(self.send, C)]

    def got_core(self, got):
        self.pair = lambda r, columns: f32(self.keep[r][..., columns]) + f32(got[r][..., columns])

    def axis(self):
        one = lambda r, columns: self.pair(r, columns).astype(BF)
        return [(one(3, LEFT), X), (one(2, LEFT), X), (one(3, RIGHT), Y), (one(1, RIGHT), Y)]

    def got_axis(self, *got):
        self.got = got

    def other(self):
        return [((self.pair(1, LEFT) + f32(self.got[0])).astype(BF), Y), ((self.pair(2, RIGHT) + f32(self.got[2])).astype(BF), X)]

    def got_other(self, left, right):
        self.left = self.pair(0, LEFT) + f32(self.got[1]) + f32(left)
        self.right = self.pair(0, RIGHT) + f32(self.got[3]) + f32(right)

    def z(self):
        return [(side[j].astype(BF), 2 * j) for side in (self.left, self.right) for j in (1, 2, 3)]

    def got_z(self, *rest):
        total = lambda side, some: (side[0] + sum(f32(r) for r in some)).astype(BF)
        self.sum = jnp.concatenate([total(self.left, rest[:3]), total(self.right, rest[3:])], 1)


class DownSum:
    def __init__(self, parts, spot):
        self.parts, self.spot = parts, spot

    def core(self):
        return [(self.parts[1], C), (self.parts[3], C)]

    def got_core(self, mine, low):
        self.mine = mine
        self.to_low = (f32(self.parts[2]) + f32(low)).astype(BF).reshape(2, 1600, 256)

    def low(self, n):
        return [(self.to_low[n], ZL)]

    def got_low(self, *got):
        q = self.spot[0]
        quarters = lambda a: a.reshape(4, 2, 400, 256)
        pick = lambda a, r, side: f32(lax.dynamic_index_in_dim(quarters(a), r ^ q, 0, False)[side])

        def lows(r, side):
            both = [g.reshape(2, 2, 400, 256) for g in got]
            at = r ^ q
            return f32(jnp.where(at < 2, *[lax.dynamic_index_in_dim(b, at & 1, 0, False)[side] for b in both]))

        self.pair = lambda r, side: pick(self.parts[0], r, side) + pick(self.mine, r, side) + lows(r, side)

    def axis(self):
        one = lambda r, side: self.pair(r, side).astype(BF)
        return [(one(3, 0), X), (one(2, 0), X), (one(3, 1), Y), (one(1, 1), Y)]

    def got_axis(self, *got):
        self.got = got

    def other(self):
        return [((self.pair(1, 0) + f32(self.got[0])).astype(BF), Y), ((self.pair(2, 1) + f32(self.got[2])).astype(BF), X)]

    def got_other(self, first, second):
        total = jnp.stack([self.pair(0, 0) + f32(self.got[1]) + f32(first), self.pair(0, 1) + f32(self.got[3]) + f32(second)])
        self.half = lambda h: lax.dynamic_index_in_dim(total, h ^ self.spot[1], 0, False)

    def high(self):
        return [(self.half(1).astype(BF), ZH)]

    def got_high(self, got):
        self.block = (self.half(0) + f32(got)).astype(BF).reshape(4, 100, 256)

    def rows(self):
        pick = lambda n: lax.dynamic_index_in_dim(self.block, n ^ self.spot[2], 0, False)
        self.own = pick(0)
        return [(pick(n), n) for n in (1, 2, 3)]

    def got_rows(self, *rest):
        stacked = jnp.stack((self.own,) + rest)
        self.sum = jnp.concatenate([lax.dynamic_index_in_dim(stacked, n ^ self.spot[2], 0, False) for n in range(4)], 1)


def solution(mesh):
    def step(x, dy, *arrays):
        weights, m, v = (arrays[i : i + 3] for i in (0, 3, 6))
        index = lax.axis_index("dp")
        q, zh, p = index >> 3, (index >> 2) & 1, index & 3
        z, c = (index >> 1) & 3, index & 1
        spot = (q, zh, p)
        ids = iter(range(100))

        columns = weights[2].reshape(2, 100, 4, 256).transpose(2, 0, 1, 3)
        part = lambda n: lax.dynamic_index_in_dim(columns, n ^ p, 0, False)
        h0, dh = x[0], dy[0]
        a0 = normed(h0)
        own_g, own_u = weights[0][1], weights[1][1]
        g0, u0, t1, t2, t3, *along = only(
            [
                wide_gather(weights[0][0], X, Y, [0, 2, 4, 6]),
                wide_gather(weights[1][0], Y, X, [1, 3, 5, 7]),
                Swap(*[(part(n), n) for n in (1, 2, 3)], step=1),
                Swap(*[(w, 2 * n) for w in (own_g, own_u) for n in (1, 2, 3)], step=3),
            ],
            next(ids), "fetch",
        )
        ordered = lambda parts, me: jnp.stack([lax.dynamic_index_in_dim(jnp.stack(parts), n ^ me, 0, False) for n in range(len(parts))])
        line_g, line_u = ordered([own_g, *along[:3]], z), ordered([own_u, *along[3:]], z)
        stacked = jnp.stack([part(0), t1, t2, t3])
        turned_down = jnp.concatenate([lax.dynamic_index_in_dim(stacked, n ^ p, 0, False) for n in range(4)], 1)

        at = jnp.arange(D)
        k, r, j, i = at >> 9, (at >> 7) & 3, (at >> 5) & 3, at & 31
        source = (r ^ q) * 256 + (j ^ z) * 64 + (k ^ c) * 32 + i
        order = (source[:, None] == jnp.arange(D)[None, :]).astype(BF)
        turned = lambda a: jnp.einsum("pk,tk->pt", order, a, preferred_element_type=F32).astype(BF)

        act0, s0, t0, d0, gx, gy, gc, uy, ux, uc = gate_up(
            a0, [g0], [u0],
            [
                down_gather(turned_down[0], X, Y, [0, 4, 11, 15, 19]),
                Swap((line_g, X), (line_g, Y), (line_g, C), step=0),
                Swap((line_u, Y), (line_u, X), (line_u, C), step=12),
            ],
            next(ids),
        )
        h1, a1, g3, gxc, gyc, g3c, u3, uyc, uxc, u3c = down(
            act0, h0, d0, [Finish({X: gx, Y: gy}, X, Y, [0, 7]), Finish({X: ux, Y: uy}, Y, X, [0, 7])], next(ids)
        )
        g1 = [line_g, gc, gy, gyc, gx, gxc, g3, g3c]
        u1 = [line_u, uc, uy, uyc, ux, uxc, u3, u3c]
        at0, at1 = turned(a0), turned(a1)
        act1, s1, t1, d1 = gate_up(a1, g1, u1, [down_gather(turned_down[1], Y, X, [0, 4, 8, 15, 19])], next(ids))

        def under(kernel, *args, n, during, name=None):
            pairs = [send() for send, _ in during]
            flat = [pair for some in pairs for pair in some]
            comms = [Swap(*flat)] if flat else []
            out = list(kernel(*args, comms, next(ids)) if name is None else only(comms, next(ids), name))
            at = n
            for some, (_, give) in zip(pairs, during):
                give(*out[at : at + len(some)])
                at += len(some)
            return out[:n]

        lows = {}

        def low(one, n):
            def got(a):
                lows.setdefault(one, []).append(a)
                if n:
                    one.got_low(*lows[one])

            return (lambda: one.low(n)), got

        go = lambda one, name: (getattr(one, name), getattr(one, "got_" + name))
        D1 = DownSum(under(by_down, act1, dh, n=4, during=[]), spot)
        dg, du = under(by_hidden, dh, s1, t1, d1, n=2, during=[go(D1, "core")])
        G1 = WideSum(*under(by_wide, at1, dg, n=2, during=[low(D1, 0)]))
        U1 = WideSum(*under(by_wide, at1, du, n=2, during=[low(D1, 1), go(G1, "core")]))
        (dh,) = under(by_input, dg, du, dh, h1, g1, u1, n=1, during=[go(G1, "axis"), go(U1, "core"), go(D1, "axis")])
        D0 = DownSum(under(by_down, act0, dh, n=4, during=[go(G1, "other"), go(U1, "axis")]), spot)
        dg, du = under(by_hidden, dh, s0, t0, d0, n=2, during=[go(D0, "core"), go(G1, "z"), go(U1, "other"), go(D1, "other")])
        G0 = WideSum(*under(by_wide, at0, dg, n=2, during=[low(D0, 0), go(D1, "high")]))
        U0 = WideSum(*under(by_wide, at0, du, n=2, during=[low(D0, 1), go(G0, "core"), go(D1, "rows")]))
        under(None, n=0, name="tail_1", during=[go(U0, "core"), go(G0, "axis"), go(U1, "z"), go(D0, "axis")])
        under(None, n=0, name="tail_2", during=[go(U0, "axis"), go(G0, "other"), go(D0, "other")])
        under(None, n=0, name="tail_3", during=[go(U0, "other"), go(G0, "z"), go(D0, "high")])
        under(None, n=0, name="tail_4", during=[go(U0, "z"), go(D0, "rows")])

        sums = [[f32(one.sum) for one in layer] for layer in ((G0, U0, D0), (G1, U1, D1))]
        squares = everyone(sum(jnp.sum(g * g) for layer in sums for g in layer), next(ids))
        factor = jnp.minimum(1.0, 0.5 * lax.rsqrt(squares / (6 * D * F) + 1e-30))
        new = []
        for i in range(3):
            g = jnp.stack([sums[0][i], sums[1][i]]) * factor
            new.append(adamw(weights[i].astype(F32), m[i], v[i], g))
        return tuple(one[which] for which in range(3) for one in new)

    states, cut = P(("rep", "dp"), None, None), P(None, "dp", None)
    return jax.shard_map(
        step,
        mesh=mesh,
        in_specs=(states, states) + (cut,) * 9,
        out_specs=(P("rep", "dp", None),) * 9,
        check_vma=False,
    )
```

time: 1320 us -> 777 us (0.59)
  Pallas kernels: 0 us -> 628 us
  waiting for transfers between devices: 591 us -> 0 us
  matrix products: 378 us -> 15 us
  blocking collectives: 276 us -> 0 us
  other arithmetic: 17.3 us -> 82.5 us
    pallas_call x0 -> x18, Pallas kernels: none -> 628 us  [the longest x5 193 us: only(): return call(*operands)]
    dot_general x15 -> x2, matrix products: 378 us -> 15 us  [step(): jnp.einsum('pk,tk->pt', order, a, preferred_element_type=F32).astype(BF)]
    all_gather x6 -> x0, waiting for transfers between devices: 346 us -> none  [fetched(): lax.all_gather(w[number], 'dp', axis=0, tiled=True)]
    reduce_scatter x4 -> x0, waiting for transfers between devices: 241 us -> none  [step(): lax.psum_scatter(by_w[name], 'dp', scatter_dimension=0, tiled=True)]
    unnamed x1 -> x0, blocking collectives: 239 us -> none
    convert_element_type x2 -> x46, other arithmetic: 4.64 us -> 60 us  [the longest x16 13.8 us: axis(): one = lambda r, columns: self.pair(r, columns).astype(BF)]
    psum x1 -> x0, blocking collectives: 36.9 us -> none  [step(): squares = lax.psum(sum((jnp.sum(g * g) for g in gradients)), 'dp')]
    another operation x0 -> x17, other arithmetic: none -> 17.3 us
  transfers between devices with their start and end apart: 14 -> 0, of which waited for: 10 -> 0; matrix products, arithmetic and copies ran while one was open for 39% -> 0% of each run, Pallas kernels for 0% -> 0%
where the time goes in v1:
time: 777 us; the launch traced here: 771 us
  Pallas kernels  628 us (81%)
  other arithmetic  82.5 us (11%)
  local copies, waits for them, and re-layouts  38.2 us (5%)
  matrix products  15 us (2%)
    pallas_call x5, Pallas kernels, only(): return call(*operands)  193 us
    pallas_call x2, Pallas kernels, gate_up(): return call(*operands)  127 us
    pallas_call x4, Pallas kernels, by_wide(): return call(*operands)  104 us
    pallas_call x2, Pallas kernels, by_hidden(): return call(*operands)  74.5 us
    pallas_call x2, Pallas kernels, by_down(): return call(*operands)  51.5 us
    pallas_call x1, Pallas kernels, by_input(): return call(*operands)  41 us
    pallas_call x1, Pallas kernels, down(): return call(*operands)  26.3 us

profile of v1, /device:TPU:0, one launch (start us, length us, event | category | flops | bytes accessed | tf_op | source)
XLA Modules:
  0.0 770.5 jit_solution(15803943296166739735)
XLA Ops:
  0.7 1.3 reshape.692
  6.4 80.3 %fetch.1 = (bf16[4,2,4,32,3200]{4,3,2,1,0:T(8,128)(2,1)}, bf16[4,2,4,32,3200]{4,3,2,1,0:T(8,128)(2,1)}, bf16[2,100,256]{2,1,0:T(8,128)(2,1)}, bf16[2,100,256]{2,...) custom-call(bf16[32,3200]{1,0:T(8,128)(2,1)} %get-tuple-element.407., ...), custom_call_target="tpu_custom_call" | custom-call | tf_op jit(solution)/shard_map/fetch/pallas_call | solution.py:431
  86.8 1.3 pad_maximum_fusion.2
  92.9 2.7 fusion.1.refs_0_
  95.6 68.6 %gate_up.2 = (bf16[2048,3200]{1,0:T(8,128)(2,1)}, f32[2048,3200]{1,0:T(8,128)}, f32[2048,3200]{1,0:T(8,128)}, bf16[2,2,4,2,400,256]{5,4,3,2,1,0:T(8,128)(2,1)}, ...) custom-call(bf16[2048,1024]{1,0:T(8,128)(2,1)} %fusion.1.refs_0_, ...), custom_call_target="tpu_custom_call" | custom-call | flops 26843545600 | bytes 78643200 | tf_op jit(solution)/shard_map/gate_up/pallas_call | solution.py:305
  164.2 26.3 %down.1 = (bf16[2048,1024]{1,0:T(8,128)(2,1)}, bf16[2048,1024]{1,0:T(8,128)(2,1)}, bf16[4,32,3200]{2,1,0:T(8,128)(2,1)}, bf16[4,32,3200]{2,1,0:T(8,128)(2,1)}, b...) custom-call(bf16[2048,3200]{1,0:T(8,128)(2,1)} %get-tuple-element.15, ...), custom_call_target="tpu_custom_call" | custom-call | flops 13421772800 | bytes 32243712 | tf_op jit(solution)/shard_map/down/pallas_call | solution.py:334
  190.5 58.4 %gate_up.3 = (bf16[2048,3200]{1,0:T(8,128)(2,1)}, f32[2048,3200]{1,0:T(8,128)}, f32[2048,3200]{1,0:T(8,128)}, bf16[2,2,4,2,400,256]{5,4,3,2,1,0:T(8,128)(2,1)}) custom-call(bf16[2048,1024]{1,0:T(8,128)(2,1)} %get-tuple-element.162.refs_0_, bf16[4,32,3200]{2,1,0:T(8,128)(2,1)} %pad_maximum_fusion.1.refs_4_.refs_5_.refs_6_.refs_1_, ...), custom_call_target="tpu_custom_call" | custom-call | flops 26843545600 | bytes 78643200 | tf_op jit(solution)/shard_map/gate_up/pallas_call | solution.py:305
  248.9 18.7 %by_down.2 = (bf16[3200,256]{1,0:T(8,128)(2,1)}, bf16[3200,256]{1,0:T(8,128)(2,1)}, bf16[3200,256]{1,0:T(8,128)(2,1)}, bf16[3200,256]{1,0:T(8,128)(2,1)}) custom-call(bf16[2048,3200]{1,0:T(8,128)(2,1)} %get-tuple-element.176.refs_0_, bf16[2048,1024]{1,0:T(8,128)(2,1)} %bitcast.321), custom_call_target="tpu_custom_call" | custom-call | flops 13421772800 | bytes 23855104 | tf_op jit(solution)/shard_map/by_down/pallas_call | solution.py:426
  267.6 36.7 %by_hidden.2 = (bf16[2048,3200]{1,0:T(8,128)(2,1)}, bf16[2048,3200]{1,0:T(8,128)(2,1)}, bf16[3200,256]{1,0:T(8,128)(2,1)}, bf16[3200,256]{1,0:T(8,128)(2,1)}) custom-call(bf16[2048,1024]{1,0:T(8,128)(2,1)} %bitcast.322, f32[2048,3200]{1,0:T(8,128)} %get-tuple-element.173.refs_1_, f32[2048,3200]{1,0:T(8,128)} %get-tuple-element.174.refs_2_, ...), custom_call_target="tpu_custom_call" | custom-call | flops 13421772800 | bytes 89391104 | tf_op jit(solution)/shard_map/by_hidden/pallas_call | solution.py:356
  304.3 1.8 add_convert_fusion.1
  306.2 1.3 fusion.88
  307.5 8.8 %fusion.5.refs_0_ = bf16[1024,2048]{1,0:T(8,128)(2,1)} fusion(bf16[2048,1024]{1,0:T(8,128)(2,1)} %get-tuple-element.162.refs_0_, s32[1024]{0:T(1024)S(1)} %and_add_fusion), kind=kOutput, calls=%fused_computation.8 | convolution fusion | flops 4298113024 | bytes 8392704 | tf_op jit(solution)/shard_map/pk,tk->pt/dot_general | solution.py:603
  316.3 24.4 %by_wide.4 = (bf16[512,3200]{1,0:T(8,128)(2,1)}, bf16[512,3200]{1,0:T(8,128)(2,1)}, bf16[1600,256]{1,0:T(8,128)(2,1)}) custom-call(bf16[1024,2048]{1,0:T(8,128)(2,1)} %fusion.5.refs_0_, bf16[2048,3200]{1,0:T(8,128)(2,1)} %get-tuple-element.179.refs_1_.refs_0_, bf16[1600,256]{1,0:T(8,128)(2,1)} %get-tuple-element.374.refs_2_), custom_call_target="tpu_custom_call" | custom-call | flops 13421772800 | bytes 23855104 | tf_op jit(solution)/shard_map/by_wide/pallas_call | solution.py:408
  340.7 24.1 %by_wide.5 = (bf16[512,3200]{1,0:T(8,128)(2,1)}, bf16[512,3200]{1,0:T(8,128)(2,1)}, bf16[1600,256]{1,0:T(8,128)(2,1)}, bf16[4,4,32,3200]{3,2,1,0:T(8,128)(2,1)}) custom-call(bf16[1024,2048]{1,0:T(8,128)(2,1)} %fusion.5.refs_0_, bf16[2048,3200]{1,0:T(8,128)(2,1)} %get-tuple-element.180.refs_1_, bf16[1600,256]{1,0:T(8,128)(2,1)} %get-tuple-element.375.refs_2_, ...), custom_call_target="tpu_custom_call" | custom-call | flops 13421772800 | bytes 23855104 | tf_op jit(solution)/shard_map/by_wide/pallas_call | solution.py:408
  364.8 2.9 fusion.56
  368.9 1.4 copy-done.5
  374.9 41.0 %by_input.1 = (bf16[2048,1024]{1,0:T(8,128)(2,1)}, bf16[4,32,1664]{2,1,0:T(8,128)(2,1)}, bf16[4,32,1664]{2,1,0:T(8,128)(2,1)}, bf16[4,32,1536]{2,1,0:T(8,128)(2,...) custom-call(bf16[2048,3200]{1,0:T(8,128)(2,1)} %get-tuple-element.17, ...), custom_call_target="tpu_custom_call" | custom-call | flops 26843545600 | bytes 51904512 | tf_op jit(solution)/shard_map/by_input/pallas_call | solution.py:390
  416.0 2.4 fusion.43
  418.4 3.2 slice_bitcast_fusion.4
  428.0 32.8 %by_down.3 = (bf16[3200,256]{1,0:T(8,128)(2,1)}, bf16[3200,256]{1,0:T(8,128)(2,1)}, bf16[3200,256]{1,0:T(8,128)(2,1)}, bf16[3200,256]{1,0:T(8,128)(2,1)}, bf16[4...) custom-call(bf16[2048,3200]{1,0:T(8,128)(2,1)} %get-tuple-element.15, ...), custom_call_target="tpu_custom_call" | custom-call | flops 13421772800 | bytes 23855104 | tf_op jit(solution)/shard_map/by_down/pallas_call | solution.py:426
  460.9 2.0 add_convert_fusion.20.refs_13_
  462.9 1.9 add_convert_fusion.8.refs_12_
  468.5 37.8 %by_hidden.3 = (bf16[2048,3200]{1,0:T(8,128)(2,1)}, bf16[2048,3200]{1,0:T(8,128)(2,1)}, bf16[3200,256]{1,0:T(8,128)(2,1)}, bf16[3200,256]{1,0:T(8,128)(2,1)}, bf...) custom-call(bf16[2048,1024]{1,0:T(8,128)(2,1)} %get-tuple-element.19, ...), custom_call_target="tpu_custom_call" | custom-call | flops 13421772800 | bytes 89391104 | tf_op jit(solution)/shard_map/by_hidden/pallas_call | solution.py:356
  506.4 1.7 fusion.42
  508.9 2.5 add_convert_fusion
  511.4 1.3 fusion.87
  512.6 6.2 fusion.4.refs_0_
  518.8 27.7 %by_wide.6 = (bf16[512,3200]{1,0:T(8,128)(2,1)}, bf16[512,3200]{1,0:T(8,128)(2,1)}, bf16[1600,256]{1,0:T(8,128)(2,1)}, bf16[400,256]{1,0:T(8,128)(2,1)}) custom-call(bf16[1024,2048]{1,0:T(8,128)(2,1)} %fusion.4.refs_0_, bf16[2048,3200]{1,0:T(8,128)(2,1)} %get-tuple-element.209.refs_1_, bf16[1600,256]{1,0:T(8,128)(2,1)} %get-tuple-element.372.refs_2_, ...), custom_call_target="tpu_custom_call" | custom-call | flops 13421772800 | bytes 23855104 | tf_op jit(solution)/shard_map/by_wide/pallas_call | solution.py:408
  548.3 27.7 %by_wide.7 = (bf16[512,3200]{1,0:T(8,128)(2,1)}, bf16[512,3200]{1,0:T(8,128)(2,1)}, bf16[1600,256]{1,0:T(8,128)(2,1)}, bf16[4,4,32,3200]{3,2,1,0:T(8,128)(2,1)},...) custom-call(bf16[1024,2048]{1,0:T(8,128)(2,1)} %fusion.4.refs_0_, ...), custom_call_target="tpu_custom_call" | custom-call | flops 13421772800 | bytes 23855104 | tf_op jit(solution)/shard_map/by_wide/pallas_call | solution.py:408
  576.1 2.9 fusion.60
  580.9 1.2 fusion.80
  589.6 30.8 %tail_1.1 = (bf16[4,4,32,3200]{3,2,1,0:T(8,128)(2,1)}, bf16[4,32,1664]{2,1,0:T(8,128)(2,1)}, bf16[4,32,1664]{2,1,0:T(8,128)(2,1)}, bf16[4,32,1536]{2,1,0:T(8,128...) custom-call(bf16[4,4,32,3200]{3,2,1,0:T(8,128)(2,1)} %bitcast.340, ...), custom_call_target="tpu_custom_call" | custom-call | tf_op jit(solution)/shard_map/tail_1/pallas_call | solution.py:431
  620.4 2.8 fusion.37
  623.2 1.9 add_convert_fusion.15.refs_5_
  626.2 2.0 copy-done.3
  632.9 33.4 %tail_2.1 = (bf16[4,32,1664]{2,1,0:T(8,128)(2,1)}, bf16[4,32,1664]{2,1,0:T(8,128)(2,1)}, bf16[4,32,1536]{2,1,0:T(8,128)(2,1)}, bf16[4,32,1536]{2,1,0:T(8,128)(2,...) custom-call(bf16[4,32,1664]{2,1,0:T(8,128)(2,1)} %add_convert_fusion, ...), custom_call_target="tpu_custom_call" | custom-call | tf_op jit(solution)/shard_map/tail_2/pallas_call | solution.py:431
  666.4 2.1 fusion.36
  674.9 29.1 %tail_3.1 = (bf16[4,32,1664]{2,1,0:T(8,128)(2,1)}, bf16[4,32,1536]{2,1,0:T(8,128)(2,1)}, bf16[32,1664]{1,0:T(8,128)(2,1)}, bf16[32,1664]{1,0:T(8,128)(2,1)}, bf1...) custom-call(bf16[4,32,1664]{2,1,0:T(8,128)(2,1)} %add_convert_fusion, ...), custom_call_target="tpu_custom_call" | custom-call | tf_op jit(solution)/shard_map/tail_3/pallas_call | solution.py:431
  712.6 2.1 fusion.76
  716.4 19.8 %tail_4.1 = (bf16[32,1664]{1,0:T(8,128)(2,1)}, bf16[32,1664]{1,0:T(8,128)(2,1)}, bf16[32,1664]{1,0:T(8,128)(2,1)}, bf16[32,1536]{1,0:T(8,128)(2,1)}, bf16[32,153...) custom-call(bf16[32,1664]{1,0:T(8,128)(2,1)} %get-tuple-element.386., ...), custom_call_target="tpu_custom_call" | custom-call | tf_op jit(solution)/shard_map/tail_4/pallas_call | solution.py:431
  748.1 10.6 %everyone.1 = f32[8,128]{1,0:T(8,128)} custom-call(f32[8,128]{1,0:T(8,128)} %broadcast_in_dim.2.value_ref), custom_call_target="tpu_custom_call" | custom-call | tf_op jit(solution)/shard_map/everyone/pallas_call | solution.py:462
  758.8 1.2 slice.951
  760.7 2.2 fusion.10
  763.0 1.5 copy.38
  764.5 1.5 copy.39
  766.0 1.2 copy.37
  767.2 1.5 fusion.18
  768.8 1.5 fusion.15
  (271 shorter events, 67.3 us)
Async XLA Ops:
  0.7 5.0 copy-start.36
  267.6 36.7 %copy-start.38 = (bf16[3200,256]{1,0:T(8,128)(2,1)S(1)}, bf16[3200,256]{1,0:T(8,128)(2,1)}, u32[]{:S(2)}) copy-start(bf16[3200,256]{1,0:T(8,128)(2,1)} %get-tuple-element.182) | copy-start | bytes 4915204
  340.7 24.1 %copy-start.28 = (bf16[1600,256]{1,0:T(8,128)(2,1)S(1)}, bf16[1600,256]{1,0:T(8,128)(2,1)}, u32[]{:S(2)}) copy-start(bf16[1600,256]{1,0:T(8,128)(2,1)} %get-tuple-element.190) | copy-start | bytes 2457604
  340.7 24.1 %copy-start.40 = (bf16[3200,256]{1,0:T(8,128)(2,1)S(1)}, bf16[3200,256]{1,0:T(8,128)(2,1)}, u32[]{:S(2)}) copy-start(bf16[3200,256]{1,0:T(8,128)(2,1)} %get-tuple-element.188) | copy-start | bytes 4915204
  374.9 41.0 %copy-start.30 = (bf16[1600,256]{1,0:T(8,128)(2,1)S(1)}, bf16[1600,256]{1,0:T(8,128)(2,1)}, u32[]{:S(2)}) copy-start(bf16[1600,256]{1,0:T(8,128)(2,1)} %get-tuple-element.191) | copy-start | bytes 2457604
  422.7 5.3 copy-start.26
  422.7 4.3 copy-start.17
  422.7 4.3 copy-start.19
  422.7 4.3 copy-start.62
  428.0 35.0 %copy-start.25 = (bf16[4,32,3200]{2,1,0:T(8,128)(2,1)S(1)}, bf16[4,32,3200]{2,1,0:T(8,128)(2,1)}, u32[]{:S(2)}) copy-start(bf16[4,32,3200]{2,1,0:T(8,128)(2,1)} %copy-done.24) | copy-start | bytes 2457604
  428.0 35.0 %copy-start.27 = (bf16[128,3200]{1,0:T(8,128)(2,1)S(1)}, bf16[128,3200]{1,0:T(8,128)(2,1)}, u32[]{:S(2)}) copy-start(bf16[128,3200]{1,0:T(8,128)(2,1)} %copy-done.26) | copy-start | bytes 2457604
  460.9 5.8 copy-start.57
  460.9 5.8 copy-start.60
  468.5 37.9 %copy-start.29 = (bf16[1600,256]{1,0:T(8,128)(2,1)S(1)}, bf16[1600,256]{1,0:T(8,128)(2,1)}, u32[]{:S(2)}) copy-start(bf16[1600,256]{1,0:T(8,128)(2,1)} %get-tuple-element.190) | copy-start | bytes 2457604
  468.5 37.9 %copy-start.31 = (bf16[1600,256]{1,0:T(8,128)(2,1)S(1)}, bf16[1600,256]{1,0:T(8,128)(2,1)}, u32[]{:S(2)}) copy-start(bf16[1600,256]{1,0:T(8,128)(2,1)} %get-tuple-element.191) | copy-start | bytes 2457604
  468.5 37.9 %copy-start.75 = (bf16[400,256]{1,0:T(8,128)(2,1)S(1)}, bf16[400,256]{1,0:T(8,128)(2,1)}, u32[]{:S(2)}) copy-start(bf16[400,256]{1,0:T(8,128)(2,1)} %get-tuple-element.212) | copy-start | bytes 614404
  468.5 37.9 %copy-start.76 = (bf16[400,256]{1,0:T(8,128)(2,1)S(1)}, bf16[400,256]{1,0:T(8,128)(2,1)}, u32[]{:S(2)}) copy-start(bf16[400,256]{1,0:T(8,128)(2,1)} %get-tuple-element.214) | copy-start | bytes 614404
  548.3 27.7 %copy-start.32 = (bf16[1600,256]{1,0:T(8,128)(2,1)S(1)}, bf16[1600,256]{1,0:T(8,128)(2,1)}, u32[]{:S(2)}) copy-start(bf16[1600,256]{1,0:T(8,128)(2,1)} %get-tuple-element.228) | copy-start | bytes 2457604
  548.3 27.7 %copy-start.39 = (bf16[3200,256]{1,0:T(8,128)(2,1)S(1)}, bf16[3200,256]{1,0:T(8,128)(2,1)}, u32[]{:S(2)}) copy-start(bf16[3200,256]{1,0:T(8,128)(2,1)} %get-tuple-element.226) | copy-start | bytes 4915204
  576.1 4.8 copy-start.55
  576.1 4.8 copy-start.56
  620.4 4.7 copy-start.64
  620.4 5.6 copy-start.8
  630.4 36.1 %copy-start.77 = (bf16[400,256]{1,0:T(8,128)(2,1)S(1)}, bf16[400,256]{1,0:T(8,128)(2,1)}, u32[]{:S(2)}) copy-start(bf16[400,256]{1,0:T(8,128)(2,1)} %get-tuple-element.242) | copy-start | bytes 614404
  666.4 4.8 copy-start.66
  673.1 32.1 %copy-start.90 = (bf16[100,256]{1,0:T(8,128)(2,1)S(1)}, bf16[100,256]{1,0:T(8,128)(2,1)}, u32[]{:S(2)}) copy-start(bf16[100,256]{1,0:T(8,128)(2,1)} %get-tuple-element.278) | copy-start | bytes 153604
  673.1 32.1 %copy-start.91 = (bf16[100,256]{1,0:T(8,128)(2,1)S(1)}, bf16[100,256]{1,0:T(8,128)(2,1)}, u32[]{:S(2)}) copy-start(bf16[100,256]{1,0:T(8,128)(2,1)} %get-tuple-element.279) | copy-start | bytes 153604
  673.1 32.1 %copy-start.92 = (bf16[100,256]{1,0:T(8,128)(2,1)S(1)}, bf16[100,256]{1,0:T(8,128)(2,1)}, u32[]{:S(2)}) copy-start(bf16[100,256]{1,0:T(8,128)(2,1)} %get-tuple-element.280) | copy-start | bytes 153604
  674.2 32.5 %copy-start.84 = (bf16[32,1664]{1,0:T(8,128)(2,1)S(1)}, bf16[32,1664]{1,0:T(8,128)(2,1)}, u32[]{:S(2)}) copy-start(bf16[32,1664]{1,0:T(8,128)(2,1)} %get-tuple-element.272) | copy-start | bytes 319492
  674.2 32.5 %copy-start.85 = (bf16[32,1664]{1,0:T(8,128)(2,1)S(1)}, bf16[32,1664]{1,0:T(8,128)(2,1)}, u32[]{:S(2)}) copy-start(bf16[32,1664]{1,0:T(8,128)(2,1)} %get-tuple-element.273) | copy-start | bytes 319492
  674.9 34.8 %copy-start.81 = (bf16[32,1664]{1,0:T(8,128)(2,1)S(1)}, bf16[32,1664]{1,0:T(8,128)(2,1)}, u32[]{:S(2)}) copy-start(bf16[32,1664]{1,0:T(8,128)(2,1)} %get-tuple-element.252) | copy-start | bytes 319492
  674.9 34.8 %copy-start.82 = (bf16[32,1664]{1,0:T(8,128)(2,1)S(1)}, bf16[32,1664]{1,0:T(8,128)(2,1)}, u32[]{:S(2)}) copy-start(bf16[32,1664]{1,0:T(8,128)(2,1)} %get-tuple-element.253) | copy-start | bytes 319492
  674.9 34.8 %copy-start.83 = (bf16[32,1664]{1,0:T(8,128)(2,1)S(1)}, bf16[32,1664]{1,0:T(8,128)(2,1)}, u32[]{:S(2)}) copy-start(bf16[32,1664]{1,0:T(8,128)(2,1)} %get-tuple-element.254) | copy-start | bytes 319492
  704.0 8.6 %copy-start.11 = (bf16[128,3200]{1,0:T(8,128)(2,1)S(1)}, bf16[128,3200]{1,0:T(8,128)(2,1)}, u32[]{:S(2)}) copy-start(bf16[128,3200]{1,0:T(8,128)(2,1)} %get-tuple-element.340) | copy-start | bytes 2457604
  705.2 7.4 copy-start.59
  706.7 8.7 %copy-start.68 = (bf16[4,32,1536]{2,1,0:T(8,128)(2,1)S(1)}, bf16[4,32,1536]{2,1,0:T(8,128)(2,1)}, u32[]{:S(2)}) copy-start(bf16[4,32,1536]{2,1,0:T(8,128)(2,1)} %get-tuple-element.260) | copy-start | bytes 1179652
  706.7 8.7 %copy-start.72 = (bf16[4,32,1536]{2,1,0:T(8,128)(2,1)S(1)}, bf16[4,32,1536]{2,1,0:T(8,128)(2,1)}, u32[]{:S(2)}) copy-start(bf16[4,32,1536]{2,1,0:T(8,128)(2,1)} %get-tuple-element.261) | copy-start | bytes 1179652
  715.6 26.3 %copy-start.89 = (bf16[32,1536]{1,0:T(8,128)(2,1)S(1)}, bf16[32,1536]{1,0:T(8,128)(2,1)}, u32[]{:S(2)}) copy-start(bf16[32,1536]{1,0:T(8,128)(2,1)} %get-tuple-element.249) | copy-start | bytes 294916
  715.6 45.0 %copy-start.33 = (bf16[2,100,1024]{2,0,1:T(2,128)(2,1)S(1)}, bf16[2,100,1024]{2,0,1:T(2,128)(2,1)}, u32[]{:S(2)}) copy-start(bf16[2,100,1024]{2,0,1:T(2,128)(2,1)} %param.15) | copy-start | bytes 1228804
  715.7 45.0 %copy-start.45 = (f32[2,100,1024]{2,0,1:T(2,128)S(1)}, f32[2,100,1024]{2,0,1:T(2,128)}, u32[]{:S(2)}) copy-start(f32[2,100,1024]{2,0,1:T(2,128)} %param.21) | copy-start | bytes 2457604
  715.7 45.0 %copy-start.51 = (bf16[1,100,256]{2,1,0:T(8,128)(2,1)S(1)}, bf16[1,100,256]{2,1,0:T(8,128)(2,1)}, u32[]{:S(2)}) copy-start(bf16[1,100,256]{2,1,0:T(8,128)(2,1)} %copy-done.50) | copy-start | bytes 153604
  715.7 45.0 %copy-start.53 = (bf16[1,100,256]{2,1,0:T(8,128)(2,1)S(1)}, bf16[1,100,256]{2,1,0:T(8,128)(2,1)}, u32[]{:S(2)}) copy-start(bf16[1,100,256]{2,1,0:T(8,128)(2,1)} %copy-done.52) | copy-start | bytes 153604
  760.7 6.5 copy-start.35
  760.7 6.5 copy-start.42
  760.7 6.5 copy-start.46
  760.7 6.5 copy-start.47
  764.5 4.3 copy-start.48
  764.5 4.3 copy-start.49
  (45 other events, 132.6 us)

commit v2 on v1

--- a/solution.py
+++ b/solution.py
@@ -59,9 +59,12 @@
     def rounds(ins, outs):
         (own,), (buf,) = ins, outs
         part = lambda r, k: buf.at[r, k]
+        here = at_peer(0, ZL, ZH)
+        there = [at_peer(2 * j, ZL, ZH) for j in (1, 2, 3)]
+        over = lambda r, bit: [(buf.at[0, 0, j], buf.at[r, 0, j], bit) for j in there]
         return [
-            [(own, buf.at[0, 0, at_peer(0, ZL, ZH)], 2 * j) for j in (1, 2, 3)],
-            [(part(0, 0), part(a, 0), first), (part(0, 0), part(b, 0), second), (part(0, 0), part(0, 1), C)],
+            [(own, buf.at[0, 0, here], 2 * j) for j in (1, 2, 3)] + [(own, buf.at[a, 0, here], first), (own, buf.at[b, 0, here], second)],
+            over(a, first) + over(b, second) + [(part(0, 0), part(0, 1), C)],
             [(part(a, 0), part(3, 0), second), (part(a, 0), part(a, 1), C), (part(b, 0), part(b, 1), C)],
             [(part(3, 0), part(3, 1), C)],
         ]
@@ -70,6 +73,7 @@
 
 
 def down_gather(own, first, second, steps):
+    lined = len(own.shape) == 3
     a, b = R[first], R[second]
 
     def rounds(ins, outs):
@@ -77,15 +81,15 @@
         part = lambda l, k, r: buf.at[l, k, r]
         across = lambda l, *rs: [(part(l, 0, r), part(l, 1, r), C) for r in rs]
         over = lambda *rs: [(part(0, 0, r), part(1, 0, r), ZL) for r in rs]
-        return [
-            [(own, buf.at[0, 0, 0, at_peer(0, ZH, ZH)], ZH)],
+        start = [] if lined else [[(own, buf.at[0, 0, 0, at_peer(0, ZH, ZH)], ZH)]]
+        return start + [
             [(part(0, 0, 0), part(0, 0, a), first), (part(0, 0, 0), part(0, 0, b), second)] + over(0) + across(0, 0),
             [(part(0, 0, a), part(0, 0, 3), second)] + over(a, b) + across(0, a, b) + across(1, 0),
             over(3) + across(0, 3) + across(1, a, b),
             across(1, 3),
         ]
 
-    return Gather(own, (2, 2, 4, 2, 400, 256), rounds, steps, lambda buf: buf.at[0, 0, 0, at_peer(0, ZH, ZH)])
+    return Gather(own, (2, 2, 4, 2, 400, 256), rounds, steps, lambda buf: buf.at[0, 0, 0] if lined else buf.at[0, 0, 0, at_peer(0, ZH, ZH)])
 
 
 class Swap:
@@ -97,6 +101,16 @@
 
     def place(self, ins, outs, scratch):
         pass
+
+
+class Halves(Swap):
+    def __init__(self, line, first, second, steps):
+        self.ins, self.steps, self.scratch = [line], steps, []
+        self.outs = [jax.ShapeDtypeStruct(line.shape, BF)] * 3
+        self.rounds = lambda i, o: [
+            [(i[0].at[:2], o[0].at[:2], first), (i[0].at[:2], o[1].at[:2], second)],
+            [(i[0].at[2:], o[0].at[2:], first), (i[0].at[2:], o[1].at[2:], second), (i[0], o[2], C)],
+        ]
 
 
 class Finish(Swap):
@@ -431,39 +445,172 @@
     return call(*operands)
 
 
-def everyone(value, number):
+class Copies:
+    def __init__(self, send, recv):
+        self.send, self.recv, self.n = send, recv, 0
+
+    def __call__(self, source, target, bits):
+        copy = pltpu.make_async_remote_copy(
+            src_ref=source, dst_ref=target, send_sem=self.send.at[self.n], recv_sem=self.recv.at[self.n],
+            device_id={"dp": peer(bits)}, device_id_type=pl.DeviceIdType.MESH,
+        )
+        copy.start()
+        self.n += 1
+        return copy
+
+
+def meet(bits):
+    barrier = pltpu.get_barrier_semaphore()
+    for b in bits:
+        pl.semaphore_signal(barrier, inc=1, device_id={"dp": peer(b)}, device_id_type=pl.DeviceIdType.MESH)
+    pl.semaphore_wait(barrier, len(bits))
+
+
+VMEM = pl.BlockSpec(memory_space=pltpu.VMEM)
+
+
+def everyone(value, pieces, number):
     groups = (tuple(range(1, 8)), (8, 16, 24))
 
-    def kernel(value_ref, out_ref, mid_ref, slots, send, recv):
-        barrier = pltpu.get_barrier_semaphore()
-        for b in groups[0] + groups[1]:
-            pl.semaphore_signal(barrier, inc=1, device_id={"dp": peer(b)}, device_id_type=pl.DeviceIdType.MESH)
-        pl.semaphore_wait(barrier, 10)
+    def kernel(value_ref, p1, p2, p3, out_ref, o1, o2, o3, mid_ref, slots, send, recv):
+        meet(groups[0] + groups[1])
+        begin = Copies(send, recv)
         source, target, n = value_ref, mid_ref, 0
+        rest = []
         for group in groups:
-            copies = []
-            for b in group:
-                copies.append(
-                    pltpu.make_async_remote_copy(
-                        src_ref=source, dst_ref=slots.at[n], send_sem=send.at[n], recv_sem=recv.at[n],
-                        device_id={"dp": peer(b)}, device_id_type=pl.DeviceIdType.MESH,
-                    )
-                )
-                copies[-1].start()
+            copies = [begin(source, slots.at[n + i], b) for i, b in enumerate(group)]
+            if not rest:
+                rest = [begin(a, b, bits) for a, b, bits in ((p1, o1, 1), (p2, o2, 2), (p3, o3, 3))]
+            total = source[...]
+            for copy in copies:
+                copy.wait()
+                total = total + slots[n]
                 n += 1
-            total = source[...]
-            for i, copy in enumerate(copies):
-                copy.wait()
-                total = total + slots[n - len(copies) + i]
             target[...] = total
             source, target = mid_ref, out_ref
-
-    spec = pl.BlockSpec(memory_space=pltpu.VMEM)
-    return pl.pallas_call(
-        kernel, in_specs=[spec], out_specs=spec, out_shape=struct((8, 128), F32),
-        scratch_shapes=[pltpu.VMEM((8, 128), F32), pltpu.VMEM((10, 8, 128), F32)] + [pltpu.SemaphoreType.DMA((10,))] * 2,
+        for copy in rest:
+            copy.wait()
+
+    call = pl.pallas_call(
+        kernel, in_specs=[VMEM] + [ANY] * 3, out_specs=[VMEM] + [ANY] * 3,
+        out_shape=[struct((8, 128), F32)] + [struct(a.shape) for a in pieces],
+        scratch_shapes=[pltpu.VMEM((8, 128), F32), pltpu.VMEM((10, 8, 128), F32)] + [pltpu.SemaphoreType.DMA((13,))] * 2,
         compiler_params=pltpu.CompilerParams(collective_id=number, has_side_effects=True), name="everyone",
-    )(jnp.broadcast_to(value, (8, 128)))[0, 0]
+    )
+    total, *got = call(jnp.broadcast_to(value, (8, 128)), *pieces)
+    return total[0, 0], got
+
+
+def tail(wides, pair, swaps, number):
+    n, width, ns = 5, 640, len(swaps)
+    ways = ((X, Y), (Y, X))
+
+    def kernel(*refs):
+        keeps, sends, pd = refs[:2], refs[2:4], refs[4]
+        swap_in, refs = refs[5 : 5 + ns], refs[5 + ns :]
+        outs, out_d, swap_out, refs = refs[:2], refs[2], refs[3 : 3 + ns], refs[3 + ns :]
+        got, snd1, rcv1, snd2, rcv2, tot, snd3, rcv3, sd1, rd1, sd2, rd2, td, sd3, rd3, send, recv = refs
+        begin = Copies(send, recv)
+        at = lambda u: slice(u * width, (u + 1) * width)
+        meet((C, X, Y, 2, 4, 6))
+        core = [[begin(sends[w].at[:, at(u)], got.at[w, u], C) for w in range(2)] for u in range(n)]
+        others = [begin(a, b, bits) for a, b, (_, bits) in zip(swap_in, swap_out, swaps)]
+        first, second, last, down1, down2, down3 = {}, {}, {}, {}, {}, []
+
+        def term(w, u, r):
+            rows = slice(r * 128, r * 128 + 128)
+            return f32(keeps[w][rows, at(u)]) + f32(got[w, u, rows, :])
+
+        def axis(u):
+            for w, (one, _) in enumerate(ways):
+                core[u][w].wait()
+                snd1[w, u, 0] = term(w, u, 3).astype(BF)
+                snd1[w, u, 1] = term(w, u, R[one]).astype(BF)
+            for i in range(2):
+                for w, (one, _) in enumerate(ways):
+                    first[w, u, i] = begin(snd1.at[w, u, i], rcv1.at[w, u, i], one)
+
+        def other(u):
+            for w, (_, two) in enumerate(ways):
+                first[w, u, 0].wait()
+                snd2[w, u] = (term(w, u, R[two]) + f32(rcv1[w, u, 0])).astype(BF)
+            for w, (_, two) in enumerate(ways):
+                second[w, u] = begin(snd2.at[w, u], rcv2.at[w, u], two)
+
+        def line(u):
+            for w in range(2):
+                first[w, u, 1].wait()
+                second[w, u].wait()
+                total = term(w, u, 0) + f32(rcv1[w, u, 1]) + f32(rcv2[w, u])
+                tot[w, u] = total[:32]
+                for j in (1, 2, 3):
+                    snd3[w, u, j - 1] = total[32 * j : 32 * j + 32].astype(BF)
+            for w in range(2):
+                last[w, u] = [begin(snd3.at[w, u, j - 1], rcv3.at[w, u, j - 1], 2 * j) for j in (1, 2, 3)]
+
+        def end(u):
+            for w in range(2):
+                total = tot[w, u]
+                for i, copy in enumerate(last[w, u]):
+                    copy.wait()
+                    total = total + f32(rcv3[w, u, i])
+                outs[w][:, at(u)] = total.astype(BF)
+
+        def down_axis():
+            for w, (one, _) in enumerate(ways):
+                sd1[w, 0] = pd[3, w].astype(BF)
+                sd1[w, 1] = pd[R[one], w].astype(BF)
+            for w, (one, _) in enumerate(ways):
+                down1[w] = [begin(sd1.at[w, i], rd1.at[w, i], one) for i in range(2)]
+
+        def down_other():
+            for w, (_, two) in enumerate(ways):
+                down1[w][0].wait()
+                sd2[w] = (pd[R[two], w] + f32(rd1[w, 0])).astype(BF)
+            for w, (_, two) in enumerate(ways):
+                down2[w] = begin(sd2.at[w], rd2.at[w], two)
+
+        def down_line():
+            for w in range(2):
+                down1[w][1].wait()
+                down2[w].wait()
+                td[w] = pd[0, w] + f32(rd1[w, 1]) + f32(rd2[w])
+            sd3[...] = td[at_peer(ZH, ZH, ZH)].astype(BF)
+            down3.append(begin(sd3, rd3, ZH))
+
+        for s in range(n + 3):
+            if s < n:
+                axis(s)
+            if s == 1:
+                down_axis()
+            if 0 <= s - 1 < n:
+                other(s - 1)
+            if s == 3:
+                down_other()
+            if 0 <= s - 2 < n:
+                line(s - 2)
+            if s == 4:
+                down_line()
+            if 0 <= s - 3 < n:
+                end(s - 3)
+        down3[0].wait()
+        out_d[...] = (td[at_peer(0, ZH, ZH)] + f32(rd3[...])).astype(BF)
+        for copy in others:
+            copy.wait()
+
+    vm = lambda *shape: pltpu.VMEM(shape, BF)
+    total = n * 2 * 7 + 7 + ns
+    call = pl.pallas_call(
+        kernel, in_specs=[VMEM] * 2 + [ANY] * 2 + [VMEM] + [ANY] * ns, out_specs=[VMEM] * 3 + [ANY] * ns,
+        out_shape=[struct((32, F))] * 2 + [struct((400, 256))] + [struct(a.shape) for a, _ in swaps],
+        scratch_shapes=[
+            vm(2, n, 512, width), vm(2, n, 2, 128, width), vm(2, n, 2, 128, width), vm(2, n, 128, width), vm(2, n, 128, width),
+            pltpu.VMEM((2, n, 32, width), F32), vm(2, n, 3, 32, width), vm(2, n, 3, 32, width),
+            vm(2, 2, 400, 256), vm(2, 2, 400, 256), vm(2, 400, 256), vm(2, 400, 256), pltpu.VMEM((2, 400, 256), F32), vm(400, 256), vm(400, 256),
+        ] + [pltpu.SemaphoreType.DMA((total,))] * 2,
+        compiler_params=pltpu.CompilerParams(collective_id=number, has_side_effects=True), name="tail",
+    )
+    return call(*[w.keep.reshape(512, F) for w in wides], *[w.send.reshape(512, F) for w in wides], pair, *[a for a, _ in swaps])
 
 
 def adamw(w, m, v, g):
@@ -602,12 +749,13 @@
         order = (source[:, None] == jnp.arange(D)[None, :]).astype(BF)
         turned = lambda a: jnp.einsum("pk,tk->pt", order, a, preferred_element_type=F32).astype(BF)
 
-        act0, s0, t0, d0, gx, gy, gc, uy, ux, uc = gate_up(
+        act0, s0, t0, d0, gx, gy, gc, uy, ux, uc, other_d = gate_up(
             a0, [g0], [u0],
             [
-                down_gather(turned_down[0], X, Y, [0, 4, 11, 15, 19]),
-                Swap((line_g, X), (line_g, Y), (line_g, C), step=0),
-                Swap((line_u, Y), (line_u, X), (line_u, C), step=12),
+                down_gather(turned_down[0], X, Y, [0, 4, 9, 16, 19]),
+                Halves(line_g, X, Y, [0, 10]),
+                Swap((line_u, Y), (line_u, X), (line_u, C), step=11),
+                Swap((turned_down[1], ZH), step=10),
             ],
             next(ids),
         )
@@ -617,7 +765,7 @@
         g1 = [line_g, gc, gy, gyc, gx, gxc, g3, g3c]
         u1 = [line_u, uc, uy, uyc, ux, uxc, u3, u3c]
         at0, at1 = turned(a0), turned(a1)
-        act1, s1, t1, d1 = gate_up(a1, g1, u1, [down_gather(turned_down[1], Y, X, [0, 4, 8, 15, 19])], next(ids))
+        act1, s1, t1, d1 = gate_up(a1, g1, u1, [down_gather(ordered([turned_down[1], other_d], zh), Y, X, [0, 5, 12, 18])], next(ids))
 
         def under(kernel, *args, n, during, name=None):
             pairs = [send() for send, _ in during]
@@ -649,14 +797,16 @@
         D0 = DownSum(under(by_down, act0, dh, n=4, during=[go(G1, "other"), go(U1, "axis")]), spot)
         dg, du = under(by_hidden, dh, s0, t0, d0, n=2, during=[go(D0, "core"), go(G1, "z"), go(U1, "other"), go(D1, "other")])
         G0 = WideSum(*under(by_wide, at0, dg, n=2, during=[low(D0, 0), go(D1, "high")]))
-        U0 = WideSum(*under(by_wide, at0, du, n=2, during=[low(D0, 1), go(G0, "core"), go(D1, "rows")]))
-        under(None, n=0, name="tail_1", during=[go(U0, "core"), go(G0, "axis"), go(U1, "z"), go(D0, "axis")])
-        under(None, n=0, name="tail_2", during=[go(U0, "axis"), go(G0, "other"), go(D0, "other")])
-        under(None, n=0, name="tail_3", during=[go(U0, "other"), go(G0, "z"), go(D0, "high")])
-        under(None, n=0, name="tail_4", during=[go(U0, "z"), go(D0, "rows")])
-
+        U0 = WideSum(*under(by_wide, at0, du, n=2, during=[low(D0, 1), go(D1, "rows")]))
+        pair = jnp.stack([jnp.stack([D0.pair(r, side) for side in range(2)]) for r in range(4)])
+        G0.sum, U0.sum, block, *rest = tail((G0, U0), pair, U1.z(), next(ids))
+        U1.got_z(*rest)
+        D0.block = block.reshape(4, 100, 256)
+        rows = D0.rows()
+        squares = sum(jnp.sum(f32(one) ** 2) for one in (G0.sum, U0.sum, block, G1.sum, U1.sum, D1.sum))
+        squares, got = everyone(squares, [a for a, _ in rows], next(ids))
+        D0.got_rows(*got)
         sums = [[f32(one.sum) for one in layer] for layer in ((G0, U0, D0), (G1, U1, D1))]
-        squares = everyone(sum(jnp.sum(g * g) for layer in sums for g in layer), next(ids))
         factor = jnp.minimum(1.0, 0.5 * lax.rsqrt(squares / (6 * D * F) + 1e-30))
         new = []
         for i in range(3):

time: 777 us -> 712 us (0.916)
  Pallas kernels: 628 us -> 597 us
  other arithmetic: 82.5 us -> 57.8 us
  local copies, waits for them, and re-layouts: 38.2 us -> 30 us
    pallas_call x5 -> x1, Pallas kernels: 193 us -> 76.2 us  [only(): return call(*operands)]
    pallas_call x1 -> x2, Pallas kernels: 10.6 us -> 104 us  [the longest x1 93.3 us: tail(): call(*[w.keep.reshape(512, F) for w in wides], *[w.send.reshape(512, F) f...]
where the time goes in v2:
time: 712 us; the launch traced here: 706 us
  Pallas kernels  597 us (84%)
  other arithmetic  57.8 us (8%)
  local copies, waits for them, and re-layouts  30 us (4%)
  matrix products  14.8 us (2%)
    pallas_call x2, Pallas kernels, gate_up(): return call(*operands)  121 us
    pallas_call x4, Pallas kernels, by_wide(): return call(*operands)  103 us
    pallas_call x1, Pallas kernels, tail(): call(*[w.keep.reshape(512, F) for w in wides], *[w.send.reshape(512, F) f...  93.3 us
    pallas_call x1, Pallas kernels, only(): return call(*operands)  76.2 us
    pallas_call x2, Pallas kernels, by_hidden(): return call(*operands)  75.3 us
    pallas_call x2, Pallas kernels, by_down(): return call(*operands)  51.7 us
    pallas_call x1, Pallas kernels, by_input(): return call(*operands)  41.7 us
    pallas_call x1, Pallas kernels, down(): return call(*operands)  25.3 us

profile of v2, /device:TPU:0, one launch (start us, length us, event | category | flops | bytes accessed | tf_op | source)
XLA Modules:
  0.0 706.3 jit_solution(14887841317569008959)
XLA Ops:
  0.7 1.3 reshape.961
  6.4 76.2 %fetch.1 = (bf16[4,2,4,32,3200]{4,3,2,1,0:T(8,128)(2,1)}, bf16[4,2,4,32,3200]{4,3,2,1,0:T(8,128)(2,1)}, bf16[2,100,256]{2,1,0:T(8,128)(2,1)}, bf16[2,100,256]{2,...) custom-call(bf16[32,3200]{1,0:T(8,128)(2,1)} %get-tuple-element.324., ...), custom_call_target="tpu_custom_call" | custom-call | tf_op jit(solution)/shard_map/fetch/pallas_call | solution.py:445
  82.7 1.3 pad_maximum_fusion.3
  88.9 2.8 fusion.1.refs_0_
  91.7 69.1 %gate_up.2 = (bf16[2048,3200]{1,0:T(8,128)(2,1)}, f32[2048,3200]{1,0:T(8,128)}, f32[2048,3200]{1,0:T(8,128)}, bf16[2,2,4,2,400,256]{5,4,3,2,1,0:T(8,128)(2,1)}, ...) custom-call(bf16[2048,1024]{1,0:T(8,128)(2,1)} %fusion.1.refs_0_, ...), custom_call_target="tpu_custom_call" | custom-call | flops 26843545600 | bytes 78643200 | tf_op jit(solution)/shard_map/gate_up/pallas_call | solution.py:319
  162.7 25.3 %down.1 = (bf16[2048,1024]{1,0:T(8,128)(2,1)}, bf16[2048,1024]{1,0:T(8,128)(2,1)}, bf16[4,32,3200]{2,1,0:T(8,128)(2,1)}, bf16[4,32,3200]{2,1,0:T(8,128)(2,1)}, b...) custom-call(bf16[2048,3200]{1,0:T(8,128)(2,1)} %get-tuple-element.12, ...), custom_call_target="tpu_custom_call" | custom-call | flops 13421772800 | bytes 32243712 | tf_op jit(solution)/shard_map/down/pallas_call | solution.py:348
  188.0 51.5 %gate_up.3 = (bf16[2048,3200]{1,0:T(8,128)(2,1)}, f32[2048,3200]{1,0:T(8,128)}, f32[2048,3200]{1,0:T(8,128)}, bf16[2,2,4,2,400,256]{5,4,3,2,1,0:T(8,128)(2,1)}) custom-call(bf16[2048,1024]{1,0:T(8,128)(2,1)} %get-tuple-element.134.refs_0_, bf16[4,32,3200]{2,1,0:T(8,128)(2,1)} %pad_maximum_fusion.2.refs_4_.refs_1_, ...), custom_call_target="tpu_custom_call" | custom-call | flops 26843545600 | bytes 78643200 | tf_op jit(solution)/shard_map/gate_up/pallas_call | solution.py:319
  239.6 18.7 %by_down.2 = (bf16[3200,256]{1,0:T(8,128)(2,1)}, bf16[3200,256]{1,0:T(8,128)(2,1)}, bf16[3200,256]{1,0:T(8,128)(2,1)}, bf16[3200,256]{1,0:T(8,128)(2,1)}) custom-call(bf16[2048,3200]{1,0:T(8,128)(2,1)} %get-tuple-element.149.refs_0_, bf16[2048,1024]{1,0:T(8,128)(2,1)} %bitcast.228), custom_call_target="tpu_custom_call" | custom-call | flops 13421772800 | bytes 23855104 | tf_op jit(solution)/shard_map/by_down/pallas_call | solution.py:440
  258.2 36.7 %by_hidden.2 = (bf16[2048,3200]{1,0:T(8,128)(2,1)}, bf16[2048,3200]{1,0:T(8,128)(2,1)}, bf16[3200,256]{1,0:T(8,128)(2,1)}, bf16[3200,256]{1,0:T(8,128)(2,1)}) custom-call(bf16[2048,1024]{1,0:T(8,128)(2,1)} %bitcast.229, f32[2048,3200]{1,0:T(8,128)} %get-tuple-element.146.refs_1_, f32[2048,3200]{1,0:T(8,128)} %get-tuple-element.147.refs_2_, ...), custom_call_target="tpu_custom_call" | custom-call | flops 13421772800 | bytes 89391104 | tf_op jit(solution)/shard_map/by_hidden/pallas_call | solution.py:370
  294.9 1.8 add_convert_fusion.1
  296.8 1.3 fusion.61
  298.1 8.6 %fusion.5.refs_0_ = bf16[1024,2048]{1,0:T(8,128)(2,1)} fusion(bf16[2048,1024]{1,0:T(8,128)(2,1)} %get-tuple-element.134.refs_0_, s32[1024]{0:T(1024)S(1)} %and_add_fusion), kind=kOutput, calls=%fused_computation.8 | convolution fusion | flops 4298113024 | bytes 8392704 | tf_op jit(solution)/shard_map/pk,tk->pt/dot_general | solution.py:750
  306.7 24.3 %by_wide.4 = (bf16[512,3200]{1,0:T(8,128)(2,1)}, bf16[512,3200]{1,0:T(8,128)(2,1)}, bf16[1600,256]{1,0:T(8,128)(2,1)}) custom-call(bf16[1024,2048]{1,0:T(8,128)(2,1)} %fusion.5.refs_0_, bf16[2048,3200]{1,0:T(8,128)(2,1)} %get-tuple-element.152.refs_1_.refs_0_, bf16[1600,256]{1,0:T(8,128)(2,1)} %get-tuple-element.294.refs_2_), custom_call_target="tpu_custom_call" | custom-call | flops 13421772800 | bytes 23855104 | tf_op jit(solution)/shard_map/by_wide/pallas_call | solution.py:422
  331.0 23.7 %by_wide.5 = (bf16[512,3200]{1,0:T(8,128)(2,1)}, bf16[512,3200]{1,0:T(8,128)(2,1)}, bf16[1600,256]{1,0:T(8,128)(2,1)}, bf16[4,4,32,3200]{3,2,1,0:T(8,128)(2,1)}) custom-call(bf16[1024,2048]{1,0:T(8,128)(2,1)} %fusion.5.refs_0_, bf16[2048,3200]{1,0:T(8,128)(2,1)} %get-tuple-element.153.refs_1_, bf16[1600,256]{1,0:T(8,128)(2,1)} %get-tuple-element.295.refs_2_, ...), custom_call_target="tpu_custom_call" | custom-call | flops 13421772800 | bytes 23855104 | tf_op jit(solution)/shard_map/by_wide/pallas_call | solution.py:422
  354.7 2.9 fusion.42
  357.7 1.1 slice_bitcast_fusion.1
  358.8 1.4 copy-done.5
  360.2 1.1 fusion.59
  364.8 41.7 %by_input.1 = (bf16[2048,1024]{1,0:T(8,128)(2,1)}, bf16[4,32,1664]{2,1,0:T(8,128)(2,1)}, bf16[4,32,1664]{2,1,0:T(8,128)(2,1)}, bf16[4,32,1536]{2,1,0:T(8,128)(2,...) custom-call(bf16[2048,3200]{1,0:T(8,128)(2,1)} %get-tuple-element.15, ...), custom_call_target="tpu_custom_call" | custom-call | flops 26843545600 | bytes 51904512 | tf_op jit(solution)/shard_map/by_input/pallas_call | solution.py:404
  406.5 2.4 fusion.33
  409.0 3.2 slice_bitcast_fusion
  412.1 1.2 fusion.58
  418.6 33.1 %by_down.3 = (bf16[3200,256]{1,0:T(8,128)(2,1)}, bf16[3200,256]{1,0:T(8,128)(2,1)}, bf16[3200,256]{1,0:T(8,128)(2,1)}, bf16[3200,256]{1,0:T(8,128)(2,1)}, bf16[4...) custom-call(bf16[2048,3200]{1,0:T(8,128)(2,1)} %get-tuple-element.12, ...), custom_call_target="tpu_custom_call" | custom-call | flops 13421772800 | bytes 23855104 | tf_op jit(solution)/shard_map/by_down/pallas_call | solution.py:440
  451.7 2.0 add_convert_fusion.8.refs_13_
  453.7 1.9 add_convert_fusion.2.refs_12_
  458.4 38.6 %by_hidden.3 = (bf16[2048,3200]{1,0:T(8,128)(2,1)}, bf16[2048,3200]{1,0:T(8,128)(2,1)}, bf16[3200,256]{1,0:T(8,128)(2,1)}, bf16[3200,256]{1,0:T(8,128)(2,1)}, bf...) custom-call(bf16[2048,1024]{1,0:T(8,128)(2,1)} %get-tuple-element.16, ...), custom_call_target="tpu_custom_call" | custom-call | flops 13421772800 | bytes 89391104 | tf_op jit(solution)/shard_map/by_hidden/pallas_call | solution.py:370
  497.1 1.9 fusion.32
  499.7 2.1 add_convert_fusion
  501.8 1.3 fusion.60
  503.0 6.2 fusion.4.refs_0_
  509.2 28.3 %by_wide.6 = (bf16[512,3200]{1,0:T(8,128)(2,1)}, bf16[512,3200]{1,0:T(8,128)(2,1)}, bf16[1600,256]{1,0:T(8,128)(2,1)}, bf16[400,256]{1,0:T(8,128)(2,1)}) custom-call(bf16[1024,2048]{1,0:T(8,128)(2,1)} %fusion.4.refs_0_, bf16[2048,3200]{1,0:T(8,128)(2,1)} %get-tuple-element.182.refs_1_, bf16[1600,256]{1,0:T(8,128)(2,1)} %get-tuple-element.293.refs_2_, ...), custom_call_target="tpu_custom_call" | custom-call | flops 13421772800 | bytes 23855104 | tf_op jit(solution)/shard_map/by_wide/pallas_call | solution.py:422
  539.2 26.6 %by_wide.7 = (bf16[512,3200]{1,0:T(8,128)(2,1)}, bf16[512,3200]{1,0:T(8,128)(2,1)}, bf16[1600,256]{1,0:T(8,128)(2,1)}, bf16[100,256]{1,0:T(8,128)(2,1)}, bf16[10...) custom-call(bf16[1024,2048]{1,0:T(8,128)(2,1)} %fusion.4.refs_0_, bf16[2048,3200]{1,0:T(8,128)(2,1)} %get-tuple-element.190.refs_1_, ...), custom_call_target="tpu_custom_call" | custom-call | flops 13421772800 | bytes 23855104 | tf_op jit(solution)/shard_map/by_wide/pallas_call | solution.py:422
  566.9 2.3 fusion.54
  569.9 1.1 fusion.55
  573.1 1.9 pad_maximum_fusion.refs_4_
  575.0 93.3 %tail.1 = (bf16[32,3200]{1,0:T(8,128)(2,1)}, bf16[32,3200]{1,0:T(8,128)(2,1)}, bf16[400,256]{1,0:T(8,128)(2,1)}, bf16[32,1664]{1,0:T(8,128)(2,1)}, bf16[32,1664]...) custom-call(bf16[512,3200]{1,0:T(8,128)(2,1)} %get-tuple-element.189, ...), custom_call_target="tpu_custom_call" | custom-call | tf_op jit(solution)/shard_map/tail/pallas_call | solution.py:613
  668.3 1.1 reshape.973
  670.9 1.1 fusion.36
  672.0 1.1 fusion.47
  674.9 1.1 fusion.49
  682.7 10.4 %everyone.1 = (f32[8,128]{1,0:T(8,128)}, bf16[100,256]{1,0:T(8,128)(2,1)}, bf16[100,256]{1,0:T(8,128)(2,1)}, bf16[100,256]{1,0:T(8,128)(2,1)}) custom-call(f32[8,128]{1,0:T(8,128)} %broadcast_in_dim.2.value_ref, bf16[100,256]{1,0:T(8,128)(2,1)} %get-tuple-element.342.p1, bf16[100,256]{1,0:T(8,128)(2,1)} %get-tuple-element.341.p2, ...), custom_call_target="tpu_custom_call" | custom-call | tf_op jit(solution)/shard_map/everyone/pallas_call | solution.py:500
  694.1 1.2 slice.660
  696.0 2.1 fusion.10
  698.1 1.5 copy.38
  699.6 1.5 copy.39
  701.1 1.2 copy.37
  702.4 1.5 fusion.18
  704.6 1.5 fusion.15
  (175 shorter events, 36.4 us)
Async XLA Ops:
  0.6 4.2 copy-start.26
  0.7 5.0 copy-start.28
  85.3 2.6 copy-start
  258.2 36.7 %copy-start.31 = (bf16[3200,256]{1,0:T(8,128)(2,1)S(1)}, bf16[3200,256]{1,0:T(8,128)(2,1)}, u32[]{:S(2)}) copy-start(bf16[3200,256]{1,0:T(8,128)(2,1)} %get-tuple-element.155) | copy-start | bytes 4915204
  331.0 23.7 %copy-start.19 = (bf16[1600,256]{1,0:T(8,128)(2,1)S(1)}, bf16[1600,256]{1,0:T(8,128)(2,1)}, u32[]{:S(2)}) copy-start(bf16[1600,256]{1,0:T(8,128)(2,1)} %get-tuple-element.163) | copy-start | bytes 2457604
  331.0 23.7 %copy-start.32 = (bf16[3200,256]{1,0:T(8,128)(2,1)S(1)}, bf16[3200,256]{1,0:T(8,128)(2,1)}, u32[]{:S(2)}) copy-start(bf16[3200,256]{1,0:T(8,128)(2,1)} %get-tuple-element.161) | copy-start | bytes 4915204
  354.7 2.9 copy-start.6
  357.7 2.5 copy-start.5
  358.8 2.5 copy-start.11
  361.3 3.5 copy-start.13
  364.8 41.7 %copy-start.21 = (bf16[1600,256]{1,0:T(8,128)(2,1)S(1)}, bf16[1600,256]{1,0:T(8,128)(2,1)}, u32[]{:S(2)}) copy-start(bf16[1600,256]{1,0:T(8,128)(2,1)} %get-tuple-element.164) | copy-start | bytes 2457604
  409.0 3.2 copy-start.4
  413.3 5.3 copy-start.17
  413.3 3.5 copy-start.47
  413.3 4.4 copy-start.12
  413.3 4.4 copy-start.14
  413.3 4.4 copy-start.46
  418.6 35.2 %copy-start.16 = (bf16[4,32,3200]{2,1,0:T(8,128)(2,1)S(1)}, bf16[4,32,3200]{2,1,0:T(8,128)(2,1)}, u32[]{:S(2)}) copy-start(bf16[4,32,3200]{2,1,0:T(8,128)(2,1)} %copy-done.15) | copy-start | bytes 2457604
  418.6 35.2 %copy-start.18 = (bf16[128,3200]{1,0:T(8,128)(2,1)S(1)}, bf16[128,3200]{1,0:T(8,128)(2,1)}, u32[]{:S(2)}) copy-start(bf16[128,3200]{1,0:T(8,128)(2,1)} %copy-done.17) | copy-start | bytes 2457604
  451.6 4.0 copy-start.9
  451.7 4.0 copy-start.10
  451.7 4.0 copy-start.48
  451.7 4.0 copy-start.49
  451.7 5.8 copy-start.44
  451.7 5.8 copy-start.45
  458.4 38.6 %copy-start.20 = (bf16[1600,256]{1,0:T(8,128)(2,1)S(1)}, bf16[1600,256]{1,0:T(8,128)(2,1)}, u32[]{:S(2)}) copy-start(bf16[1600,256]{1,0:T(8,128)(2,1)} %get-tuple-element.163) | copy-start | bytes 2457604
  458.4 38.6 %copy-start.22 = (bf16[1600,256]{1,0:T(8,128)(2,1)S(1)}, bf16[1600,256]{1,0:T(8,128)(2,1)}, u32[]{:S(2)}) copy-start(bf16[1600,256]{1,0:T(8,128)(2,1)} %get-tuple-element.164) | copy-start | bytes 2457604
  458.4 38.6 %copy-start.51 = (bf16[400,256]{1,0:T(8,128)(2,1)S(1)}, bf16[400,256]{1,0:T(8,128)(2,1)}, u32[]{:S(2)}) copy-start(bf16[400,256]{1,0:T(8,128)(2,1)} %get-tuple-element.185) | copy-start | bytes 614404
  497.1 2.6 copy-start.30
  499.7 3.3 copy-start.1
  539.2 27.6 %copy-start.7 = (bf16[4,32,3200]{2,1,0:T(8,128)(2,1)S(1)}, bf16[4,32,3200]{2,1,0:T(8,128)(2,1)}, u32[]{:S(2)}) copy-start(bf16[4,32,3200]{2,1,0:T(8,128)(2,1)} %get-tuple-element.280) | copy-start | bytes 2457604
  539.2 27.6 %copy-start.8 = (bf16[128,3200]{1,0:T(8,128)(2,1)S(1)}, bf16[128,3200]{1,0:T(8,128)(2,1)}, u32[]{:S(2)}) copy-start(bf16[128,3200]{1,0:T(8,128)(2,1)} %get-tuple-element.276) | copy-start | bytes 2457604
  565.8 4.1 copy-start.42
  565.8 4.1 copy-start.43
  566.8 5.0 copy-start.2
  566.9 4.9 copy-start.3
  566.9 4.9 copy-start.23
  566.9 4.9 copy-start.24
  668.3 8.5 %copy-start.38 = (bf16[32,3200]{1,0:T(8,128)(2,1)S(1)}, bf16[32,3200]{1,0:T(8,128)(2,1)}, u32[]{:S(2)}) copy-start(bf16[32,3200]{1,0:T(8,128)(2,1)} %get-tuple-element.203) | copy-start | bytes 614404
  668.3 8.5 %copy-start.39 = (bf16[32,3200]{1,0:T(8,128)(2,1)S(1)}, bf16[32,3200]{1,0:T(8,128)(2,1)}, u32[]{:S(2)}) copy-start(bf16[32,3200]{1,0:T(8,128)(2,1)} %get-tuple-element.210) | copy-start | bytes 614404
  668.3 10.5 %copy-start.40 = (bf16[400,256]{1,0:T(8,128)(2,1)S(1)}, bf16[400,256]{1,0:T(8,128)(2,1)}, u32[]{:S(2)}) copy-start(bf16[400,256]{1,0:T(8,128)(2,1)} %get-tuple-element.211) | copy-start | bytes 614404
  668.3 27.6 %copy-start.25 = (bf16[2,100,1024]{2,0,1:T(2,128)(2,1)S(1)}, bf16[2,100,1024]{2,0,1:T(2,128)(2,1)}, u32[]{:S(2)}) copy-start(bf16[2,100,1024]{2,0,1:T(2,128)(2,1)} %param.15) | copy-start | bytes 1228804
  668.3 27.6 %copy-start.33 = (f32[2,100,1024]{2,0,1:T(2,128)S(1)}, f32[2,100,1024]{2,0,1:T(2,128)}, u32[]{:S(2)}) copy-start(f32[2,100,1024]{2,0,1:T(2,128)} %param.21) | copy-start | bytes 2457604
  670.2 4.8 copy-start.41
  670.2 23.0 %copy-start.50 = (bf16[1,100,256]{2,1,0:T(8,128)(2,1)S(1)}, bf16[1,100,256]{2,1,0:T(8,128)(2,1)}, u32[]{:S(2)}) copy-start(bf16[1,100,256]{2,1,0:T(8,128)(2,1)} %get-tuple-element.339) | copy-start | bytes 153604
  698.0 4.4 copy-start.27
  698.0 4.4 copy-start.34
  698.0 4.4 copy-start.35
  (10 other events, 21.2 us)

commit v3 on v2

--- a/solution.py
+++ b/solution.py
@@ -111,6 +111,16 @@
             [(i[0].at[:2], o[0].at[:2], first), (i[0].at[:2], o[1].at[:2], second)],
             [(i[0].at[2:], o[0].at[2:], first), (i[0].at[2:], o[1].at[2:], second), (i[0], o[2], C)],
         ]
+
+
+def wide_half(own, first, second, steps):
+    def rounds(ins, outs):
+        (own,), (line, a, b, k) = ins, outs
+        return [[(own, line.at[at_peer(0, ZL, ZH)], 2 * j) for j in (1, 2, 3)], [(line, a, first), (line, b, second), (line, k, C)]]
+
+    half = Gather(own, (4, 32, F), rounds, steps, lambda line: line.at[at_peer(0, ZL, ZH)])
+    half.outs = half.outs * 4
+    return half
 
 
 class Finish(Swap):
@@ -734,12 +744,12 @@
                 wide_gather(weights[0][0], X, Y, [0, 2, 4, 6]),
                 wide_gather(weights[1][0], Y, X, [1, 3, 5, 7]),
                 Swap(*[(part(n), n) for n in (1, 2, 3)], step=1),
-                Swap(*[(w, 2 * n) for w in (own_g, own_u) for n in (1, 2, 3)], step=3),
+                Swap(*[(own_g, 2 * n) for n in (1, 2, 3)], step=3),
             ],
             next(ids), "fetch",
         )
         ordered = lambda parts, me: jnp.stack([lax.dynamic_index_in_dim(jnp.stack(parts), n ^ me, 0, False) for n in range(len(parts))])
-        line_g, line_u = ordered([own_g, *along[:3]], z), ordered([own_u, *along[3:]], z)
+        line_g = ordered([own_g, *along], z)
         stacked = jnp.stack([part(0), t1, t2, t3])
         turned_down = jnp.concatenate([lax.dynamic_index_in_dim(stacked, n ^ p, 0, False) for n in range(4)], 1)
 
@@ -749,12 +759,12 @@
         order = (source[:, None] == jnp.arange(D)[None, :]).astype(BF)
         turned = lambda a: jnp.einsum("pk,tk->pt", order, a, preferred_element_type=F32).astype(BF)
 
-        act0, s0, t0, d0, gx, gy, gc, uy, ux, uc, other_d = gate_up(
+        act0, s0, t0, d0, gx, gy, gc, line_u, uy, ux, uc, other_d = gate_up(
             a0, [g0], [u0],
             [
                 down_gather(turned_down[0], X, Y, [0, 4, 9, 16, 19]),
                 Halves(line_g, X, Y, [0, 10]),
-                Swap((line_u, Y), (line_u, X), (line_u, C), step=11),
+                wide_half(own_u, Y, X, [3, 12]),
                 Swap((turned_down[1], ZH), step=10),
             ],
             next(ids),

time: 712 us -> 722 us (1.014)
  Pallas kernels: 597 us -> 608 us
    pallas_call x2, Pallas kernels: 121 us -> 132 us  [gate_up(): return call(*operands)]
where the time goes in v3:
time: 722 us; the launch traced here: 716 us
  Pallas kernels  608 us (84%)
  other arithmetic  56.6 us (8%)
  local copies, waits for them, and re-layouts  29.9 us (4%)
  matrix products  14.8 us (2%)
    pallas_call x2, Pallas kernels, gate_up(): return call(*operands)  132 us
    pallas_call x4, Pallas kernels, by_wide(): return call(*operands)  104 us
    pallas_call x1, Pallas kernels, tail(): call(*[w.keep.reshape(512, F) for w in wides], *[w.send.reshape(512, F) f...  92.8 us
    pallas_call x1, Pallas kernels, only(): return call(*operands)  75.4 us
    pallas_call x2, Pallas kernels, by_hidden(): return call(*operands)  74.8 us
    pallas_call x2, Pallas kernels, by_down(): return call(*operands)  51.8 us
    pallas_call x1, Pallas kernels, by_input(): return call(*operands)  41.5 us
    pallas_call x1, Pallas kernels, down(): return call(*operands)  25.4 us

profile of v3, /device:TPU:0, one launch (start us, length us, event | category | flops | bytes accessed | tf_op | source)
XLA Modules:
  0.0 715.6 jit_solution(10854604335738413293)
XLA Ops:
  0.7 1.3 reshape.961
  6.4 75.4 %fetch.1 = (bf16[4,2,4,32,3200]{4,3,2,1,0:T(8,128)(2,1)}, bf16[4,2,4,32,3200]{4,3,2,1,0:T(8,128)(2,1)}, bf16[2,100,256]{2,1,0:T(8,128)(2,1)}, bf16[2,100,256]{2,...) custom-call(bf16[32,3200]{1,0:T(8,128)(2,1)} %get-tuple-element.315., ...), custom_call_target="tpu_custom_call" | custom-call | tf_op jit(solution)/shard_map/fetch/pallas_call | solution.py:455
  81.8 1.3 pad_maximum_fusion.1
  86.7 2.8 fusion.1.refs_0_
  89.5 82.0 %gate_up.2 = (bf16[2048,3200]{1,0:T(8,128)(2,1)}, f32[2048,3200]{1,0:T(8,128)}, f32[2048,3200]{1,0:T(8,128)}, bf16[2,2,4,2,400,256]{5,4,3,2,1,0:T(8,128)(2,1)}, ...) custom-call(bf16[2048,1024]{1,0:T(8,128)(2,1)} %fusion.1.refs_0_, ...), custom_call_target="tpu_custom_call" | custom-call | flops 26843545600 | bytes 78643200 | tf_op jit(solution)/shard_map/gate_up/pallas_call | solution.py:329
  173.4 25.4 %down.1 = (bf16[2048,1024]{1,0:T(8,128)(2,1)}, bf16[2048,1024]{1,0:T(8,128)(2,1)}, bf16[4,32,3200]{2,1,0:T(8,128)(2,1)}, bf16[4,32,3200]{2,1,0:T(8,128)(2,1)}, b...) custom-call(bf16[2048,3200]{1,0:T(8,128)(2,1)} %get-tuple-element.12, ...), custom_call_target="tpu_custom_call" | custom-call | flops 13421772800 | bytes 32243712 | tf_op jit(solution)/shard_map/down/pallas_call | solution.py:358
  198.8 50.4 %gate_up.3 = (bf16[2048,3200]{1,0:T(8,128)(2,1)}, f32[2048,3200]{1,0:T(8,128)}, f32[2048,3200]{1,0:T(8,128)}, bf16[2,2,4,2,400,256]{5,4,3,2,1,0:T(8,128)(2,1)}) custom-call(bf16[2048,1024]{1,0:T(8,128)(2,1)} %get-tuple-element.129.refs_0_, bf16[4,32,3200]{2,1,0:T(8,128)(2,1)} %pad_maximum_fusion.2.refs_4_.refs_1_, ...), custom_call_target="tpu_custom_call" | custom-call | flops 26843545600 | bytes 78643200 | tf_op jit(solution)/shard_map/gate_up/pallas_call | solution.py:329
  249.2 18.7 %by_down.2 = (bf16[3200,256]{1,0:T(8,128)(2,1)}, bf16[3200,256]{1,0:T(8,128)(2,1)}, bf16[3200,256]{1,0:T(8,128)(2,1)}, bf16[3200,256]{1,0:T(8,128)(2,1)}) custom-call(bf16[2048,3200]{1,0:T(8,128)(2,1)} %get-tuple-element.145.refs_0_, bf16[2048,1024]{1,0:T(8,128)(2,1)} %bitcast.225), custom_call_target="tpu_custom_call" | custom-call | flops 13421772800 | bytes 23855104 | tf_op jit(solution)/shard_map/by_down/pallas_call | solution.py:450
  267.9 36.7 %by_hidden.2 = (bf16[2048,3200]{1,0:T(8,128)(2,1)}, bf16[2048,3200]{1,0:T(8,128)(2,1)}, bf16[3200,256]{1,0:T(8,128)(2,1)}, bf16[3200,256]{1,0:T(8,128)(2,1)}) custom-call(bf16[2048,1024]{1,0:T(8,128)(2,1)} %bitcast.226, f32[2048,3200]{1,0:T(8,128)} %get-tuple-element.142.refs_1_, f32[2048,3200]{1,0:T(8,128)} %get-tuple-element.143.refs_2_, ...), custom_call_target="tpu_custom_call" | custom-call | flops 13421772800 | bytes 89391104 | tf_op jit(solution)/shard_map/by_hidden/pallas_call | solution.py:380
  304.6 1.8 add_convert_fusion.1
  306.5 1.3 fusion.61
  307.8 8.6 %fusion.5.refs_0_ = bf16[1024,2048]{1,0:T(8,128)(2,1)} fusion(bf16[2048,1024]{1,0:T(8,128)(2,1)} %get-tuple-element.129.refs_0_, s32[1024]{0:T(1024)S(1)} %and_add_fusion), kind=kOutput, calls=%fused_computation.8 | convolution fusion | flops 4298113024 | bytes 8392704 | tf_op jit(solution)/shard_map/pk,tk->pt/dot_general | solution.py:760
  316.4 24.1 %by_wide.4 = (bf16[512,3200]{1,0:T(8,128)(2,1)}, bf16[512,3200]{1,0:T(8,128)(2,1)}, bf16[1600,256]{1,0:T(8,128)(2,1)}) custom-call(bf16[1024,2048]{1,0:T(8,128)(2,1)} %fusion.5.refs_0_, bf16[2048,3200]{1,0:T(8,128)(2,1)} %get-tuple-element.148.refs_1_.refs_0_, bf16[1600,256]{1,0:T(8,128)(2,1)} %get-tuple-element.290.refs_2_), custom_call_target="tpu_custom_call" | custom-call | flops 13421772800 | bytes 23855104 | tf_op jit(solution)/shard_map/by_wide/pallas_call | solution.py:432
  340.5 25.0 %by_wide.5 = (bf16[512,3200]{1,0:T(8,128)(2,1)}, bf16[512,3200]{1,0:T(8,128)(2,1)}, bf16[1600,256]{1,0:T(8,128)(2,1)}, bf16[4,4,32,3200]{3,2,1,0:T(8,128)(2,1)}) custom-call(bf16[1024,2048]{1,0:T(8,128)(2,1)} %fusion.5.refs_0_, bf16[2048,3200]{1,0:T(8,128)(2,1)} %get-tuple-element.149.refs_1_, bf16[1600,256]{1,0:T(8,128)(2,1)} %get-tuple-element.291.refs_2_, ...), custom_call_target="tpu_custom_call" | custom-call | flops 13421772800 | bytes 23855104 | tf_op jit(solution)/shard_map/by_wide/pallas_call | solution.py:432
  365.6 2.9 fusion.42
  368.5 1.1 slice_bitcast_fusion.1
  369.7 1.4 copy-done.5
  371.1 1.1 fusion.59
  375.7 41.5 %by_input.1 = (bf16[2048,1024]{1,0:T(8,128)(2,1)}, bf16[4,32,1664]{2,1,0:T(8,128)(2,1)}, bf16[4,32,1664]{2,1,0:T(8,128)(2,1)}, bf16[4,32,1536]{2,1,0:T(8,128)(2,...) custom-call(bf16[2048,3200]{1,0:T(8,128)(2,1)} %get-tuple-element.14, ...), custom_call_target="tpu_custom_call" | custom-call | flops 26843545600 | bytes 51904512 | tf_op jit(solution)/shard_map/by_input/pallas_call | solution.py:414
  417.2 2.4 fusion.33
  419.6 3.2 slice_bitcast_fusion
  422.8 1.2 fusion.58
  429.2 33.1 %by_down.3 = (bf16[3200,256]{1,0:T(8,128)(2,1)}, bf16[3200,256]{1,0:T(8,128)(2,1)}, bf16[3200,256]{1,0:T(8,128)(2,1)}, bf16[3200,256]{1,0:T(8,128)(2,1)}, bf16[4...) custom-call(bf16[2048,3200]{1,0:T(8,128)(2,1)} %get-tuple-element.12, ...), custom_call_target="tpu_custom_call" | custom-call | flops 13421772800 | bytes 23855104 | tf_op jit(solution)/shard_map/by_down/pallas_call | solution.py:450
  462.4 2.0 add_convert_fusion.8.refs_13_
  464.4 1.9 add_convert_fusion.2.refs_12_
  469.1 38.1 %by_hidden.3 = (bf16[2048,3200]{1,0:T(8,128)(2,1)}, bf16[2048,3200]{1,0:T(8,128)(2,1)}, bf16[3200,256]{1,0:T(8,128)(2,1)}, bf16[3200,256]{1,0:T(8,128)(2,1)}, bf...) custom-call(bf16[2048,1024]{1,0:T(8,128)(2,1)} %get-tuple-element.16, ...), custom_call_target="tpu_custom_call" | custom-call | flops 13421772800 | bytes 89391104 | tf_op jit(solution)/shard_map/by_hidden/pallas_call | solution.py:380
  507.2 1.9 fusion.32
  509.9 2.1 add_convert_fusion
  511.9 1.3 fusion.60
  513.2 6.2 fusion.4.refs_0_
  519.4 27.9 %by_wide.6 = (bf16[512,3200]{1,0:T(8,128)(2,1)}, bf16[512,3200]{1,0:T(8,128)(2,1)}, bf16[1600,256]{1,0:T(8,128)(2,1)}, bf16[400,256]{1,0:T(8,128)(2,1)}) custom-call(bf16[1024,2048]{1,0:T(8,128)(2,1)} %fusion.4.refs_0_, bf16[2048,3200]{1,0:T(8,128)(2,1)} %get-tuple-element.178.refs_1_, bf16[1600,256]{1,0:T(8,128)(2,1)} %get-tuple-element.289.refs_2_, ...), custom_call_target="tpu_custom_call" | custom-call | flops 13421772800 | bytes 23855104 | tf_op jit(solution)/shard_map/by_wide/pallas_call | solution.py:432
  549.0 26.6 %by_wide.7 = (bf16[512,3200]{1,0:T(8,128)(2,1)}, bf16[512,3200]{1,0:T(8,128)(2,1)}, bf16[1600,256]{1,0:T(8,128)(2,1)}, bf16[100,256]{1,0:T(8,128)(2,1)}, bf16[10...) custom-call(bf16[1024,2048]{1,0:T(8,128)(2,1)} %fusion.4.refs_0_, bf16[2048,3200]{1,0:T(8,128)(2,1)} %get-tuple-element.186.refs_1_, ...), custom_call_target="tpu_custom_call" | custom-call | flops 13421772800 | bytes 23855104 | tf_op jit(solution)/shard_map/by_wide/pallas_call | solution.py:432
  576.7 2.3 fusion.54
  579.8 1.1 fusion.55
  582.9 1.9 pad_maximum_fusion.refs_4_
  584.8 92.8 %tail.1 = (bf16[32,3200]{1,0:T(8,128)(2,1)}, bf16[32,3200]{1,0:T(8,128)(2,1)}, bf16[400,256]{1,0:T(8,128)(2,1)}, bf16[32,1664]{1,0:T(8,128)(2,1)}, bf16[32,1664]...) custom-call(bf16[512,3200]{1,0:T(8,128)(2,1)} %get-tuple-element.185, ...), custom_call_target="tpu_custom_call" | custom-call | tf_op jit(solution)/shard_map/tail/pallas_call | solution.py:623
  677.7 1.1 reshape.973
  680.3 1.1 fusion.36
  681.4 1.1 fusion.47
  684.3 1.1 fusion.49
  692.1 10.4 %everyone.1 = (f32[8,128]{1,0:T(8,128)}, bf16[100,256]{1,0:T(8,128)(2,1)}, bf16[100,256]{1,0:T(8,128)(2,1)}, bf16[100,256]{1,0:T(8,128)(2,1)}) custom-call(f32[8,128]{1,0:T(8,128)} %broadcast_in_dim.2.value_ref, bf16[100,256]{1,0:T(8,128)(2,1)} %get-tuple-element.333.p1, bf16[100,256]{1,0:T(8,128)(2,1)} %get-tuple-element.332.p2, ...), custom_call_target="tpu_custom_call" | custom-call | tf_op jit(solution)/shard_map/everyone/pallas_call | solution.py:510
  703.4 1.2 slice.660
  705.3 2.1 fusion.10
  707.4 1.5 copy.38
  709.0 1.5 copy.39
  710.5 1.2 copy.37
  711.8 1.5 fusion.18
  714.0 1.5 fusion.15
  (166 shorter events, 35.1 us)
Async XLA Ops:
  0.6 4.2 copy-start.28
  0.7 5.0 copy-start.26
  83.2 2.6 copy-start
  267.9 36.7 %copy-start.31 = (bf16[3200,256]{1,0:T(8,128)(2,1)S(1)}, bf16[3200,256]{1,0:T(8,128)(2,1)}, u32[]{:S(2)}) copy-start(bf16[3200,256]{1,0:T(8,128)(2,1)} %get-tuple-element.151) | copy-start | bytes 4915204
  340.5 25.1 %copy-start.19 = (bf16[1600,256]{1,0:T(8,128)(2,1)S(1)}, bf16[1600,256]{1,0:T(8,128)(2,1)}, u32[]{:S(2)}) copy-start(bf16[1600,256]{1,0:T(8,128)(2,1)} %get-tuple-element.159) | copy-start | bytes 2457604
  340.5 25.1 %copy-start.32 = (bf16[3200,256]{1,0:T(8,128)(2,1)S(1)}, bf16[3200,256]{1,0:T(8,128)(2,1)}, u32[]{:S(2)}) copy-start(bf16[3200,256]{1,0:T(8,128)(2,1)} %get-tuple-element.157) | copy-start | bytes 4915204
  365.6 2.9 copy-start.6
  368.5 2.5 copy-start.5
  369.7 2.5 copy-start.11
  372.2 3.5 copy-start.13
  375.7 41.5 %copy-start.21 = (bf16[1600,256]{1,0:T(8,128)(2,1)S(1)}, bf16[1600,256]{1,0:T(8,128)(2,1)}, u32[]{:S(2)}) copy-start(bf16[1600,256]{1,0:T(8,128)(2,1)} %get-tuple-element.160) | copy-start | bytes 2457604
  419.6 3.2 copy-start.4
  423.9 5.3 copy-start.17
  423.9 3.5 copy-start.47
  423.9 4.4 copy-start.12
  423.9 4.4 copy-start.14
  423.9 4.4 copy-start.46
  429.2 35.2 %copy-start.16 = (bf16[4,32,3200]{2,1,0:T(8,128)(2,1)S(1)}, bf16[4,32,3200]{2,1,0:T(8,128)(2,1)}, u32[]{:S(2)}) copy-start(bf16[4,32,3200]{2,1,0:T(8,128)(2,1)} %copy-done.15) | copy-start | bytes 2457604
  429.2 35.2 %copy-start.18 = (bf16[128,3200]{1,0:T(8,128)(2,1)S(1)}, bf16[128,3200]{1,0:T(8,128)(2,1)}, u32[]{:S(2)}) copy-start(bf16[128,3200]{1,0:T(8,128)(2,1)} %copy-done.17) | copy-start | bytes 2457604
  462.3 4.0 copy-start.9
  462.3 4.0 copy-start.10
  462.3 4.0 copy-start.48
  462.3 4.0 copy-start.49
  462.4 5.8 copy-start.44
  462.4 5.8 copy-start.45
  469.1 38.1 %copy-start.20 = (bf16[1600,256]{1,0:T(8,128)(2,1)S(1)}, bf16[1600,256]{1,0:T(8,128)(2,1)}, u32[]{:S(2)}) copy-start(bf16[1600,256]{1,0:T(8,128)(2,1)} %get-tuple-element.159) | copy-start | bytes 2457604
  469.1 38.1 %copy-start.22 = (bf16[1600,256]{1,0:T(8,128)(2,1)S(1)}, bf16[1600,256]{1,0:T(8,128)(2,1)}, u32[]{:S(2)}) copy-start(bf16[1600,256]{1,0:T(8,128)(2,1)} %get-tuple-element.160) | copy-start | bytes 2457604
  469.1 38.1 %copy-start.51 = (bf16[400,256]{1,0:T(8,128)(2,1)S(1)}, bf16[400,256]{1,0:T(8,128)(2,1)}, u32[]{:S(2)}) copy-start(bf16[400,256]{1,0:T(8,128)(2,1)} %get-tuple-element.181) | copy-start | bytes 614404
  507.2 2.6 copy-start.30
  509.8 3.3 copy-start.1
  549.0 27.6 %copy-start.7 = (bf16[4,32,3200]{2,1,0:T(8,128)(2,1)S(1)}, bf16[4,32,3200]{2,1,0:T(8,128)(2,1)}, u32[]{:S(2)}) copy-start(bf16[4,32,3200]{2,1,0:T(8,128)(2,1)} %get-tuple-element.276) | copy-start | bytes 2457604
  549.0 27.6 %copy-start.8 = (bf16[128,3200]{1,0:T(8,128)(2,1)S(1)}, bf16[128,3200]{1,0:T(8,128)(2,1)}, u32[]{:S(2)}) copy-start(bf16[128,3200]{1,0:T(8,128)(2,1)} %get-tuple-element.272) | copy-start | bytes 2457604
  575.7 4.1 copy-start.42
  575.7 4.1 copy-start.43
  576.7 5.0 copy-start.2
  576.7 4.9 copy-start.3
  576.7 4.9 copy-start.23
  576.7 4.9 copy-start.24
  677.6 8.5 %copy-start.38 = (bf16[32,3200]{1,0:T(8,128)(2,1)S(1)}, bf16[32,3200]{1,0:T(8,128)(2,1)}, u32[]{:S(2)}) copy-start(bf16[32,3200]{1,0:T(8,128)(2,1)} %get-tuple-element.199) | copy-start | bytes 614404
  677.6 8.5 %copy-start.39 = (bf16[32,3200]{1,0:T(8,128)(2,1)S(1)}, bf16[32,3200]{1,0:T(8,128)(2,1)}, u32[]{:S(2)}) copy-start(bf16[32,3200]{1,0:T(8,128)(2,1)} %get-tuple-element.206) | copy-start | bytes 614404
  677.6 10.5 %copy-start.40 = (bf16[400,256]{1,0:T(8,128)(2,1)S(1)}, bf16[400,256]{1,0:T(8,128)(2,1)}, u32[]{:S(2)}) copy-start(bf16[400,256]{1,0:T(8,128)(2,1)} %get-tuple-element.207) | copy-start | bytes 614404
  677.7 27.7 %copy-start.25 = (bf16[2,100,1024]{2,0,1:T(2,128)(2,1)S(1)}, bf16[2,100,1024]{2,0,1:T(2,128)(2,1)}, u32[]{:S(2)}) copy-start(bf16[2,100,1024]{2,0,1:T(2,128)(2,1)} %param.15) | copy-start | bytes 1228804
  677.7 27.7 %copy-start.33 = (f32[2,100,1024]{2,0,1:T(2,128)S(1)}, f32[2,100,1024]{2,0,1:T(2,128)}, u32[]{:S(2)}) copy-start(f32[2,100,1024]{2,0,1:T(2,128)} %param.21) | copy-start | bytes 2457604
  679.5 4.8 copy-start.41
  679.5 23.0 %copy-start.50 = (bf16[1,100,256]{2,1,0:T(8,128)(2,1)S(1)}, bf16[1,100,256]{2,1,0:T(8,128)(2,1)}, u32[]{:S(2)}) copy-start(bf16[1,100,256]{2,1,0:T(8,128)(2,1)} %get-tuple-element.330) | copy-start | bytes 153604
  707.4 4.4 copy-start.27
  707.4 4.4 copy-start.34
  707.4 4.4 copy-start.35
  (7 other events, 14.2 us)
